TPU v7x, 8 devices: a whole 2x2x1 slice. The times are simulated.
8 devices in a mesh: dp: 1 (over z), tp: 8 (over y, x, core).
Axes of the slice: x: 2, y: 2, z: 1, core: 2. Of those that a mesh axis runs over, the one named last changes fastest.
Arguments:
- residual: bfloat16 [512, 1152], P('dp', 'tp')
- lengths: int32 [512], P(('dp', 'tp'))
- ln_scale: bfloat16 [2, 1152], P(None, 'tp')
- w_in: bfloat16 [2, 1152, 14848], P(None, None, 'tp')
- w_key: bfloat16 [2, 1152, 256], replicated
- w_val: bfloat16 [2, 1152, 256], replicated
- w_out: bfloat16 [2, 7936, 1152], P(None, 'tp')
- key_cache: bfloat16 [2, 512, 256, 256], P(None, ('dp', 'tp'))
- val_cache: bfloat16 [2, 512, 256, 256], P(None, ('dp', 'tp'))
Outputs:
- output 1: bfloat16 [512, 1152], P('dp', 'tp')
- output 2: bfloat16 [2, 512, 256, 256], P(None, ('dp', 'tp'))
- output 3: bfloat16 [2, 512, 256, 256], P(None, ('dp', 'tp'))
All inputs are finite; a program needn't handle non-finite values.
Results may differ from a plain program's by a relative error of at most 0.0118485.
Values are sent between devices in bfloat16 or wider.
A program may use at most 1 GiB of HBM per device.

v0:
```python
import jax
import jax.numpy as jnp
from jax import lax
from jax.sharding import PartitionSpec as P

NORM_EPS = 1e-6


def rotary(vectors, angles):
    half_dim = vectors.shape[-1] // 2
    first_half = vectors[..., :half_dim].astype(jnp.float32)
    second_half = vectors[..., half_dim:].astype(jnp.float32)
    cos_part = jnp.cos(angles)
    sin_part = jnp.sin(angles)
    return jnp.concatenate([first_half * cos_part - second_half * sin_part, second_half * cos_part + first_half * sin_part], axis=-1).astype(jnp.bfloat16)


def norm_sharded(resid_local, scale_local, full_width):
    resid_f32 = resid_local.astype(jnp.float32)
    row_stats = jnp.stack([jnp.sum(resid_f32, axis=-1), jnp.sum(resid_f32 * resid_f32, axis=-1)], axis=-1)
    row_stats = lax.psum(row_stats, "tp")
    row_mean = row_stats[:, 0:1] / full_width
    row_var = row_stats[:, 1:2] / full_width - row_mean * row_mean
    return ((resid_f32 - row_mean) * lax.rsqrt(row_var + NORM_EPS) * scale_local.astype(jnp.float32)).astype(jnp.bfloat16)


def attend(query_rows, new_key, new_val, key_cache, val_cache, lengths):
    score_scale = query_rows.shape[-1] ** -0.5
    cache_scores = jnp.einsum("bhd,bsd->bhs", query_rows, key_cache, preferred_element_type=jnp.float32) * score_scale
    positions = lax.broadcasted_iota(jnp.int32, (1, 1, key_cache.shape[1]), 2)
    cache_scores = jnp.where(positions < lengths[:, None, None], cache_scores, -1e30)
    new_scores = jnp.einsum("bhd,bd->bh", query_rows, new_key, preferred_element_type=jnp.float32) * score_scale
    row_max = jnp.maximum(jnp.max(cache_scores, axis=-1), new_scores)
    cache_weights = jnp.exp(cache_scores - row_max[:, :, None])
    new_weights = jnp.exp(new_scores - row_max)
    weight_sum = jnp.sum(cache_weights, axis=-1) + new_weights
    mixed_vals = jnp.einsum("bhs,bsd->bhd", cache_weights.astype(jnp.bfloat16), val_cache, preferred_element_type=jnp.float32)
    mixed_vals = mixed_vals + new_weights.astype(jnp.bfloat16).astype(jnp.float32)[:, :, None] * new_val.astype(jnp.float32)[:, None, :]
    return (mixed_vals / weight_sum[:, :, None]).astype(jnp.bfloat16)


def solution(mesh):
    tp_size = mesh.shape["tp"]

    def device_step(residual, lengths, ln_scale, w_in, w_key, w_val, w_out, key_cache, val_cache):
        rows_dev = lengths.shape[0]
        full_width = w_in.shape[1]
        head_dim = w_key.shape[2]
        ffn_dev = w_in.shape[2] - w_out.shape[1]
        q_dev = w_out.shape[1] - ffn_dev
        num_heads = q_dev * tp_size // head_dim
        row_start = lax.axis_index("tp") * rows_dev
        inv_freq = 10000.0 ** (-jnp.arange(head_dim // 2, dtype=jnp.float32) * (2.0 / head_dim))
        angles = lengths.astype(jnp.float32)[:, None] * inv_freq[None, :]
        new_keys = []
        new_vals = []
        for layer_idx in range(w_in.shape[0]):
            normed_local = norm_sharded(residual, ln_scale[layer_idx], full_width)
            normed = lax.all_gather(normed_local, "tp", axis=1, tiled=True)
            fused_out = jnp.dot(normed, w_in[layer_idx], preferred_element_type=jnp.float32).astype(jnp.bfloat16)
            gate_vals = fused_out[:, :ffn_dev].astype(jnp.float32)
            up_vals = fused_out[:, ffn_dev:2 * ffn_dev].astype(jnp.float32)
            activated = (jax.nn.silu(gate_vals) * up_vals).astype(jnp.bfloat16)
            query_rows = lax.all_to_all(fused_out[:, 2 * ffn_dev:], "tp", 0, 1, tiled=True)
            query_rows = rotary(query_rows.reshape(rows_dev, num_heads, head_dim), angles[:, None, :])
            own_normed = lax.dynamic_slice_in_dim(normed, row_start, rows_dev, axis=0)
            new_key = rotary(jnp.dot(own_normed, w_key[layer_idx], preferred_element_type=jnp.float32).astype(jnp.bfloat16), angles)
            new_val = jnp.dot(own_normed, w_val[layer_idx], preferred_element_type=jnp.float32).astype(jnp.bfloat16)
            attn_rows = attend(query_rows, new_key, new_val, key_cache[layer_idx], val_cache[layer_idx], lengths)
            attn_cols = lax.all_to_all(attn_rows.reshape(rows_dev, num_heads * head_dim), "tp", 1, 0, tiled=True)
            joined = jnp.concatenate([activated, attn_cols], axis=1)
            partial_sum = jnp.dot(joined, w_out[layer_idx], preferred_element_type=jnp.float32).astype(jnp.bfloat16)
            update = lax.psum_scatter(partial_sum, "tp", scatter_dimension=1, tiled=True)
            residual = (residual.astype(jnp.float32) + update.astype(jnp.float32)).astype(jnp.bfloat16)
            new_keys.append(new_key)
            new_vals.append(new_val)
        slot_mask = lax.broadcasted_iota(jnp.int32, (1, 1, key_cache.shape[2], 1), 2) == lengths[None, :, None, None]
        key_out = jnp.where(slot_mask, jnp.stack(new_keys)[:, :, None, :], key_cache)
        val_out = jnp.where(slot_mask, jnp.stack(new_vals)[:, :, None, :], val_cache)
        return residual, key_out, val_out

    cache_spec = P(None, ("dp", "tp"), None, None)
    return jax.shard_map(device_step, mesh=mesh, in_specs=(P("dp", "tp"), P(("dp", "tp")), P(None, "tp"), P(None, None, "tp"), P(), P(), P(None, "tp", None), cache_spec, cache_spec), out_specs=(P("dp", "tp"), cache_spec, cache_spec), check_vma=False)
```

profile of v0, /device:TPU:0, one launch (start us, length us, event | category | flops | bytes accessed | tf_op | source)
XLA Modules:
  0.0 238.1 jit_solution(12557300780476610582)
XLA Ops:
  7.2 1.3 slice_convert_fusion
  8.5 1.0 convert_reduce_fusion.1
  9.5 25.1 %psum.14 = f32[512,2]{0,1:T(2,128)S(1)} all-reduce(f32[512,2]{0,1:T(2,128)S(1)} %pad_maximum_fusion.7), channel_id=1, replica_groups=mesh['dp'=1,'tp'=8] {'tp'}, use_global_device_ids=true, to_apply=%region_2.0 | all-reduce | flops 1024 | bytes 8192 | tf_op jit(solution)/shard_map/psum | solution.py:21
  34.6 1.7 fusion.85
  36.3 0.7 convert_element_type.154
  37.0 1.3 iota_compare_fusion
  38.4 17.0 %all-gather.3.cloned.1.call-done = bf16[512,1152]{0,1:T(8,128)(2,1)} async-done(((bf16[512,144]{0,1:T(8,128)(2,1)}), bf16[512,1152]{0,1:T(8,128)(2,1)}) %all-gather.3.cloned.1.call-update) | async-done | bytes 1179664 | tf_op jit(solution)/shard_map/all_gather | solution.py:59
  55.4 5.2 %fusion.18 = bf16[512,1856]{0,1:T(8,128)(2,1)S(1)} fusion(bf16[512,1152]{0,1:T(8,128)(2,1)} %all-gather.3.cloned.1.call-done, bf16[2,1152,1856]{1,2,0:T(8,128)(2,1)} %param.12), kind=kOutput, calls=%fused_computation.20 | convolution fusion | flops 2190376960 | bytes 7356416 | tf_op jit(solution)/shard_map/dot_general | solution.py:60
  60.6 0.8 copy.16
  61.4 2.1 all-to-all-start
  63.5 1.4 convolution_convert_fusion.5
  64.9 2.2 fusion.148
  67.1 0.2 fusion.125
  67.3 1.4 all-to-all-done
  69.0 0.2 fusion.114
  69.2 5.8 %fusion.147 = (f32[64,4]{1,0:T(8,128)S(1)}, f32[64,4,256]{2,1,0:T(4,128)S(1)}) fusion(bf16[2,64,256,256]{3,2,1,0:T(8,128)(2,1)} %param.16, bf16[64,4,128]{2,1,0:T(4,128)(2,1)S(1)} %get-tuple-element.11, bf16[64,4,128]{2,1,0:T(4,128)(2,1)S(1)} %get-tuple-element.10, pred[64,256]{1,0:T(8,128)(4,1)S(1)} %get-tuple-element.31), kind=kOutput, calls=%fused_computation.177 | convolution fusion | flops 34012928 | bytes 8799232 | tf_op jit(solution)/shard_map/bhd,bsd->bhs/dot_general | solution.py:29
  75.0 0.2 fusion.96
  75.3 4.6 %fusion.71 = bf16[64,4,256]{2,1,0:T(4,128)(2,1)S(1)} fusion(bf16[2,64,256,256]{3,2,1,0:T(8,128)(2,1)} %param.17, f32[64,4,256]{2,1,0:T(4,128)S(1)} %get-tuple-element.33, f32[64,4]{1,0:T(8,128)S(1)} %get-tuple-element.15, f32[64,256]{1,0:T(8,128)S(1)} %copy-done.10, f32[64,4]{1,0:T(8,128)S(1)} %get-tuple-element.14, f32[64,4]{1,0:T(8,128)S(1)} %multiply_maximum_fusion.1), kind=kOutput, calls=%fused_computation.61 | convolution fusion | flops 33947648 | bytes 8850432 | tf_op jit(solution)/shard_map/bhs,bsd->bhd/dot_general | solution.py:37
  80.0 0.7 copy.18
  80.7 2.1 all-to-all-start.1
  82.8 1.5 fusion.37
  84.3 3.7 %all-to-all-done.1 = bf16[64,8,128]{2,0,1:T(8,128)(2,1)S(1)} async-done(((bf16[64,8,128]{2,0,1:T(8,128)(2,1)}), bf16[64,8,128]{2,0,1:T(8,128)(2,1)S(1)}, u32[]{:S(2)}, u32[]{:S(2)}) %all-to-all-start.1) | async-done | bytes 131104 | tf_op jit(solution)/shard_map/all_to_all | solution.py:70
  88.1 4.4 %convolution_convert_fusion.1 = bf16[512,1152]{0,1:T(8,128)(2,1)} fusion(bf16[2,992,1152]{2,1,0:T(8,128)(2,1)} %param.15, bf16[512,128]{0,1:T(8,128)(2,1)S(1)} %copy.19, bf16[512,864]{0,1:T(8,128)(2,1)} %fusion.37), kind=kOutput, calls=%fused_computation.23 | convolution fusion | flops 1172832256 | bytes 4481024 | tf_op jit(solution)/shard_map/dot_general | solution.py:72
  92.6 27.4 %reduce-scatter.3.cloned.1.call-done = bf16[512,144]{0,1:T(8,128)(2,1)} async-done(((bf16[512,1152]{0,1:T(8,128)(2,1)}), bf16[512,144]{0,1:T(8,128)(2,1)}) %reduce-scatter.3.cloned.1.call-update) | async-done | bytes 147472 | tf_op jit(solution)/shard_map/reduce_scatter | solution.py:73
  120.1 1.0 convert_reduce_fusion
  121.1 22.4 %psum.15 = f32[512,2]{0,1:T(2,128)S(1)} all-reduce(f32[512,2]{0,1:T(2,128)S(1)} %pad_maximum_fusion.8), channel_id=1, replica_groups=mesh['dp'=1,'tp'=8] {'tp'}, use_global_device_ids=true, to_apply=%region_8.9 | all-reduce | flops 1024 | bytes 8192 | tf_op jit(solution)/shard_map/psum | solution.py:21
  143.5 0.8 fusion.90
  144.3 20.0 %all-gather.5.cloned.1.call-done = bf16[512,1152]{0,1:T(8,128)(2,1)} async-done(((bf16[512,144]{0,1:T(8,128)(2,1)}), bf16[512,1152]{0,1:T(8,128)(2,1)}) %all-gather.5.cloned.1.call-update) | async-done | bytes 1179664 | tf_op jit(solution)/shard_map/all_gather | solution.py:59
  164.3 5.2 %fusion.21 = bf16[512,1856]{0,1:T(8,128)(2,1)S(1)} fusion(bf16[512,1152]{0,1:T(8,128)(2,1)} %all-gather.5.cloned.1.call-done, bf16[2,1152,1856]{1,2,0:T(8,128)(2,1)} %param.12), kind=kOutput, calls=%fused_computation.21 | convolution fusion | flops 2190376960 | bytes 7356416 | tf_op jit(solution)/shard_map/dot_general | solution.py:60
  169.5 0.6 fusion.36
  170.1 0.8 copy.20
  170.8 2.1 all-to-all-start.2
  172.9 1.4 convolution_convert_fusion.3
  174.3 1.4 fusion.150
  175.7 0.8 fusion.129
  176.6 1.6 all-to-all-done.2
  178.3 0.8 fusion.105
  179.2 5.7 %fusion.149 = (f32[64,4]{1,0:T(8,128)S(1)}, f32[64,4,256]{2,1,0:T(4,128)S(1)}) fusion(bf16[2,64,256,256]{3,2,1,0:T(8,128)(2,1)} %param.16, bf16[64,4,128]{2,1,0:T(4,128)(2,1)S(1)} %get-tuple-element.9, bf16[64,4,128]{2,1,0:T(4,128)(2,1)S(1)} %get-tuple-element.8, pred[64,256]{1,0:T(8,128)(4,1)} %copy-done.11), kind=kOutput, calls=%fused_computation.179 | convolution fusion | flops 34012928 | bytes 8799232 | tf_op jit(solution)/shard_map/bhd,bsd->bhs/dot_general | solution.py:29
  184.9 0.2 fusion.112
  185.2 0.2 fusion.98
  185.5 4.6 %fusion.65 = bf16[64,4,256]{2,1,0:T(4,128)(2,1)S(1)} fusion(bf16[2,64,256,256]{3,2,1,0:T(8,128)(2,1)} %param.17, f32[64,4,256]{2,1,0:T(4,128)S(1)} %get-tuple-element.37, f32[64,4]{1,0:T(8,128)S(1)} %get-tuple-element.13, f32[64,256]{1,0:T(8,128)S(1)} %get-tuple-element.38, f32[64,4]{1,0:T(8,128)S(1)} %get-tuple-element.12, ...), kind=kOutput, calls=%fused_computation.59 | convolution fusion | flops 33947648 | bytes 8850432 | tf_op jit(solution)/shard_map/bhs,bsd->bhd/dot_general | solution.py:37
  190.2 0.7 copy.22
  190.9 2.1 all-to-all-start.3
  193.1 5.1 %all-to-all-done.3 = bf16[64,8,128]{2,0,1:T(8,128)(2,1)S(1)} async-done(((bf16[64,8,128]{2,0,1:T(8,128)(2,1)}), bf16[64,8,128]{2,0,1:T(8,128)(2,1)S(1)}, u32[]{:S(2)}, u32[]{:S(2)}) %all-to-all-start.3) | async-done | bytes 131104 | tf_op jit(solution)/shard_map/all_to_all | solution.py:70
  198.3 4.1 %convolution_convert_fusion = bf16[512,1152]{0,1:T(8,128)(2,1)} fusion(bf16[2,992,1152]{2,1,0:T(8,128)(2,1)} %param.15, bf16[512,128]{0,1:T(8,128)(2,1)S(1)} %copy.23, bf16[512,864]{0,1:T(8,128)(2,1)S(1)} %fusion.36), kind=kOutput, calls=%fused_computation.22 | convolution fusion | flops 1172832256 | bytes 4481024 | tf_op jit(solution)/shard_map/dot_general | solution.py:72
  202.5 23.0 %broadcast_select_fusion = (bf16[2,64,256,256]{3,2,1,0:T(8,128)(2,1)}, bf16[2,64,256,256]{3,2,1,0:T(8,128)(2,1)}) fusion(bf16[2,64,256,256]{3,2,1,0:T(8,128)(2,1)} %param.17, pred[64,256]{1,0:T(8,128)(4,1)S(1)} %copy-done.9, bf16[2,64,256]{2,1,0:T(8,128)(2,1)S(1)} %get-tuple-element.41, bf16[2,64,256,256]{3,2,1,0:T(8,128)(2,1)} %param.16, ...), kind=kLoop, calls=%fused_computation | loop fusion | flops 16777216 | bytes 67256320 | tf_op jit(solution)/shard_map/jit(_where)/select_n | solution.py:79
  225.5 4.5 %reduce-scatter.5.cloned.1.call-done = bf16[512,144]{0,1:T(8,128)(2,1)} async-done(((bf16[512,1152]{0,1:T(8,128)(2,1)}), bf16[512,144]{0,1:T(8,128)(2,1)}) %reduce-scatter.5.cloned.1.call-update) | async-done | bytes 147472 | tf_op jit(solution)/shard_map/reduce_scatter | solution.py:73
  230.0 1.6 fusion.91
  (61 shorter events, 1.3 us)
Async XLA Ops:
  7.2 48.2 %all-gather.3.cloned.1.call-start = ((), (), s32[]{:S(2)}) async-start(), calls=%async_computation.6 | async-start | bytes 1327104 | tf_op jit(solution)/shard_map/all_gather | solution.py:59
  37.0 30.1 %copy-start.13 = (f32[64]{0:T(128)}, f32[64]{0:T(128)S(1)}, u32[]{:S(2)}) copy-start(f32[64]{0:T(128)S(1)} %convert_element_type.154) | copy-start | bytes 772
  37.0 30.1 %copy-start.14 = (f32[128]{0:T(128)}, f32[128]{0:T(128)S(1)}, u32[]{:S(2)}) copy-start(f32[128]{0:T(128)S(1)} %multiply_power_fusion) | copy-start | bytes 1540
  38.4 30.8 %copy-start.11 = (pred[64,256]{1,0:T(8,128)(4,1)}, pred[64,256]{1,0:T(8,128)(4,1)S(1)}, u32[]{:S(2)}) copy-start(pred[64,256]{1,0:T(8,128)(4,1)S(1)} %get-tuple-element.31) | copy-start | bytes 49156
  38.4 25.1 %copy-start.1 = (bf16[2,1152,256]{2,1,0:T(8,128)(2,1)S(1)}, bf16[2,1152,256]{2,1,0:T(8,128)(2,1)}, u32[]{:S(2)}) copy-start(bf16[2,1152,256]{2,1,0:T(8,128)(2,1)} %param.13) | copy-start | bytes 3538948
  61.4 7.3 %all-to-all-start = ((bf16[8,64,128]{2,1,0:T(8,128)(2,1)}), bf16[8,64,128]{2,1,0:T(8,128)(2,1)S(1)}, u32[]{:S(2)}, u32[]{:S(2)}) async-start(bf16[8,64,128]{2,1,0:T(8,128)(2,1)} %bitcast.6), calls=%async_computation | async-start | bytes 262144 | tf_op jit(solution)/shard_map/all_to_all | solution.py:64
  67.3 1.4 copy-start.4
  67.3 1.4 copy-start.6
  67.3 7.7 %copy-start.3 = (f32[64,128]{1,0:T(8,128)}, f32[64,128]{1,0:T(8,128)S(1)}, u32[]{:S(2)}) copy-start(f32[64,128]{1,0:T(8,128)S(1)} %get-tuple-element.29) | copy-start | bytes 98308
  69.2 6.1 %copy-start.10 = (f32[64,256]{1,0:T(8,128)S(1)}, f32[64,256]{1,0:T(8,128)}, u32[]{:S(2)}) copy-start(f32[64,256]{1,0:T(8,128)} %get-tuple-element.34) | copy-start | bytes 196612
  80.7 7.3 %all-to-all-start.1 = ((bf16[64,8,128]{2,0,1:T(8,128)(2,1)}), bf16[64,8,128]{2,0,1:T(8,128)(2,1)S(1)}, u32[]{:S(2)}, u32[]{:S(2)}) async-start(bf16[64,8,128]{2,0,1:T(8,128)(2,1)} %copy.18), calls=%async_computation.1 | async-start | bytes 262144 | tf_op jit(solution)/shard_map/all_to_all | solution.py:70
  82.8 37.3 %reduce-scatter.3.cloned.1.call-start = ((), (), s32[]{:S(2)}) async-start(), calls=%async_computation.7 | async-start | bytes 1327104 | tf_op jit(solution)/shard_map/reduce_scatter | solution.py:73
  88.1 31.9 %copy-start = (bf16[512,144]{0,1:T(8,128)(2,1)S(1)}, bf16[512,144]{0,1:T(8,128)(2,1)}, u32[]{:S(2)}) copy-start(bf16[512,144]{0,1:T(8,128)(2,1)} %param.9) | copy-start | bytes 442372
  88.1 55.4 %copy-start.12 = (f32[1,144]{1,0:T(1,128)S(1)}, f32[1,144]{1,0:T(1,128)}, u32[]{:S(2)}) copy-start(f32[1,144]{1,0:T(1,128)} %get-tuple-element.26) | copy-start | bytes 1732
  92.6 71.7 %all-gather.5.cloned.1.call-start = ((), (), s32[]{:S(2)}) async-start(), calls=%async_computation.8 | async-start | bytes 1327104 | tf_op jit(solution)/shard_map/all_gather | solution.py:59
  169.5 4.9 %copy-start.2 = (bf16[2,1152,256]{2,1,0:T(8,128)(2,1)S(1)}, bf16[2,1152,256]{2,1,0:T(8,128)(2,1)}, u32[]{:S(2)}) copy-start(bf16[2,1152,256]{2,1,0:T(8,128)(2,1)} %param.14) | copy-start | bytes 3538948
  170.8 7.3 %all-to-all-start.2 = ((bf16[8,64,128]{2,1,0:T(8,128)(2,1)}), bf16[8,64,128]{2,1,0:T(8,128)(2,1)S(1)}, u32[]{:S(2)}, u32[]{:S(2)}) async-start(bf16[8,64,128]{2,1,0:T(8,128)(2,1)} %bitcast.107), calls=%async_computation.3 | async-start | bytes 262144 | tf_op jit(solution)/shard_map/all_to_all | solution.py:64
  185.4 7.6 %copy-start.5 = (bf16[64,128]{1,0:T(8,128)(2,1)S(1)}, bf16[64,128]{1,0:T(8,128)(2,1)}, u32[]{:S(2)}) copy-start(bf16[64,128]{1,0:T(8,128)(2,1)} %copy-done.4) | copy-start | bytes 49156
  185.4 7.6 %copy-start.7 = (bf16[64,128]{1,0:T(8,128)(2,1)S(1)}, bf16[64,128]{1,0:T(8,128)(2,1)}, u32[]{:S(2)}) copy-start(bf16[64,128]{1,0:T(8,128)(2,1)} %copy-done.6) | copy-start | bytes 49156
  185.4 7.6 %copy-start.8 = (bf16[64,256]{1,0:T(8,128)(2,1)S(1)}, bf16[64,256]{1,0:T(8,128)(2,1)}, u32[]{:S(2)}) copy-start(bf16[64,256]{1,0:T(8,128)(2,1)} %get-tuple-element.35) | copy-start | bytes 98308
  190.9 7.3 %all-to-all-start.3 = ((bf16[64,8,128]{2,0,1:T(8,128)(2,1)}), bf16[64,8,128]{2,0,1:T(8,128)(2,1)S(1)}, u32[]{:S(2)}, u32[]{:S(2)}) async-start(bf16[64,8,128]{2,0,1:T(8,128)(2,1)} %copy.22), calls=%async_computation.4 | async-start | bytes 262144 | tf_op jit(solution)/shard_map/all_to_all | solution.py:70
  193.0 37.0 %reduce-scatter.5.cloned.1.call-start = ((), (), s32[]{:S(2)}) async-start(), calls=%async_computation.9 | async-start | bytes 1327104 | tf_op jit(solution)/shard_map/reduce_scatter | solution.py:73
  198.3 4.2 %copy-start.9 = (pred[64,256]{1,0:T(8,128)(4,1)S(1)}, pred[64,256]{1,0:T(8,128)(4,1)}, u32[]{:S(2)}) copy-start(pred[64,256]{1,0:T(8,128)(4,1)} %get-tuple-element.30) | copy-start | bytes 49156
Sparse Core Ops, SparseCore 0:
  36.5 18.8 all-gather.2
  92.7 27.3 reduce-scatter.2
  144.4 19.8 all-gather.4
  202.6 27.3 reduce-scatter.4
where the time goes:
time: 239 us; the launch traced here: 238 us
  waiting for transfers between devices  80.8 us (34%)
  blocking collectives  47.5 us (20%)
  matrix products  46.4 us (19%)
  other arithmetic  36.9 us (15%)
  between operations  14.2 us (6%)
  starting transfers between devices  8.59 us (4%)
  local copies, waits for them, and re-layouts  3.68 us (2%)
    psum x2, blocking collectives, norm_sharded(): row_stats = lax.psum(row_stats, 'tp')  47.5 us
    all_gather x2, waiting for transfers between devices, device_step(): normed = lax.all_gather(normed_local, 'tp', axis=1, tiled=True)  37 us
    reduce_scatter x2, waiting for transfers between devices, device_step(): lax.psum_scatter(partial_sum, 'tp', scatter_dimension=1, tiled=True)  31.9 us
    select_n x1, other arithmetic, device_step(): jnp.where(slot_mask, jnp.stack(new_vals)[:, :, None, :], val_cache)  23 us
    dot_general x2, matrix products, attend(): jnp.einsum('bhd,bsd->bhs', query_rows, key_cache, preferred_element_type=...  11.5 us
    dot_general x2, matrix products, device_step(): jnp.dot(normed, w_in[layer_idx], preferred_element_type=jnp.float32)  10.4 us
    dot_general x2, matrix products, attend(): jnp.einsum('bhs,bsd->bhd', cache_weights.astype(jnp.bfloat16), val_cache,...  9.28 us
    all_to_all x2, waiting for transfers between devices, device_step(): lax.all_to_all(attn_rows.reshape(rows_dev, num_heads * head_dim), 'tp', 1...  8.83 us
  transfers between devices with their start and end apart: 8, of which 8 were waited for; matrix products, arithmetic and copies ran while one was open for 14% of the time, Pallas kernels for 0%

commit v1 on v0

v1 whole, which is shorter than its diff:
```python
import functools

import jax
import jax.numpy as jnp
import numpy as np
from jax import lax
from jax.experimental import pallas as pl
from jax.experimental.pallas import tpu as pltpu
from jax.sharding import PartitionSpec as P

NORM_EPS = 1e-6
MESH = pl.DeviceIdType.MESH
CHUNKS = 2
BF = jnp.bfloat16
F32 = jnp.float32
TN = (((0,), (0,)), ((), ()))
NT = (((1,), (1,)), ((), ()))


def dot(a, b, dims=None):
    if dims is None:
        return jnp.dot(a, b, preferred_element_type=F32)
    return lax.dot_general(a, b, dims, preferred_element_type=F32)


def iota2(shape, dim):
    return lax.broadcasted_iota(jnp.int32, shape, dim)


def step_kernel(r_in, len_row, ln_in, inv_freq, w_in, w_key, w_val, w_out, k_cache, v_cache,
                r_out, new_k, new_v,
                w_in_v, w_key_v, w_val_v, w_out_v, k_buf, v_buf,
                r_all, ln_all, ln_col, h_t, joined, y_part, d2d, rs_recv, rs_send,
                q_send, q_recv, o_send, o_recv, q_rows, s_rows, o_rows, kv_tmp,
                cos_b, sin_b, len_col, len_rep, perm,
                w_sems, c_sems, ln_ss, ln_rs, ag_ss, ag_rs, q_ss, q_rs, o_ss, o_rs, d_ss, d_rs, t_ss, t_rs):
    layers, width = w_in.shape[0], w_in.shape[2]
    shard, batch = r_in.shape
    tp = width // shard
    rows = batch // tp
    q_dev = q_send.shape[2]
    ffn_dev = w_out.shape[1] - q_dev
    head_dim = w_key.shape[2]
    half = head_dim // 2
    heads = q_dev * tp // head_dim
    cw = batch // CHUNKS
    hw = cw // 2
    cr = rows // CHUNKS
    hr = cr * heads

    me = lax.axis_index("tp")
    core, xpos, ypos = me % 2, (me // 2) % 2, me // 4
    dp_ = me + 1 - 2 * core
    dx = me + 2 - 4 * xpos
    dy = me + 4 - 8 * ypos
    dd = dx + 4 - 8 * ypos
    flip = 1 - 2 * core

    def rcopy(src, dst, ss, rs, dev):
        return pltpu.make_async_remote_copy(src_ref=src, dst_ref=dst, send_sem=ss, recv_sem=rs,
                                            device_id={"tp": dev}, device_id_type=MESH)

    barrier = pltpu.get_barrier_semaphore()
    for off in range(1, tp):
        pl.semaphore_signal(barrier, 1, device_id={"tp": (me + off) % tp}, device_id_type=MESH)

    loads = {}

    def load(name, src, dst, sem):
        loads[name] = pltpu.make_async_copy(src, dst, sem)
        loads[name].start()

    def load_weights(l):
        load(("in", l), w_in.at[l], w_in_v.at[l], w_sems.at[l, 0])
        load(("key", l), w_key.at[l], w_key_v.at[l], w_sems.at[l, 1])
        load(("val", l), w_val.at[l], w_val_v.at[l], w_sems.at[l, 2])
        load(("out", l), w_out.at[l], w_out_v.at[l], w_sems.at[l, 3])

    def load_cache(l, c):
        load(("k", l, c), k_cache.at[l, pl.ds(c * cr, cr)], k_buf.at[pl.ds(c * cr, cr)], c_sems.at[l, c, 0])
        load(("v", l, c), v_cache.at[l, pl.ds(c * cr, cr)], v_buf.at[pl.ds(c * cr, cr)], c_sems.at[l, c, 1])

    load_weights(0)
    load_cache(0, 0)
    load_cache(0, 1)

    src_i = iota2((batch, batch), 0)
    dst_i = iota2((batch, batch), 1)
    want = ((dst_i % cw) // cr) * rows + (dst_i // cw) * cr + dst_i % cr
    perm[...] = jnp.where(src_i == want, 1.0, 0.0).astype(BF)
    r_all[0, me] = dot(r_in[...], perm[...]).astype(BF)
    ln_all[me] = ln_in[...]

    pl.semaphore_wait(barrier, tp - 1)

    sends = []

    def lanes(c, h):
        return pl.ds(c * cw + h * hw, hw)

    def ag_send(l, c, idx, dev, slot, h):
        ref = r_all.at[l, slot, :, lanes(c, h)]
        cp = rcopy(ref, ref, ag_ss.at[l, c, idx], ag_rs.at[l, c, slot, h], dev)
        cp.start()
        sends.append(cp)

    def ag_wait(l, c, slot, h):
        ref = r_all.at[l, slot, :, lanes(c, h)]
        rcopy(ref, ref, ag_ss.at[l, c, 0], ag_rs.at[l, c, slot, h], dp_).wait_recv()

    def ag_start(l, c):
        ag_send(l, c, 0, dx, me, 0)
        ag_send(l, c, 1, dy, me, 1)
        ag_send(l, c, 2, dx, me, 1)
        ag_send(l, c, 3, dy, me, 0)
        ag_send(l, c, 4, dp_, me, 0)
        ag_send(l, c, 5, dp_, me, 1)

    def ag_forward(l, c):
        ag_wait(l, c, dx, 0)
        ag_send(l, c, 6, dy, dx, 0)
        ag_send(l, c, 7, dp_, dx, 0)
        ag_wait(l, c, dy, 1)
        ag_send(l, c, 8, dx, dy, 1)
        ag_send(l, c, 9, dp_, dy, 1)

    def ag_relay(l, c):
        ag_wait(l, c, dx, 1)
        ag_send(l, c, 10, dp_, dx, 1)
        ag_wait(l, c, dy, 0)
        ag_send(l, c, 11, dp_, dy, 0)

    def ag_finish(l, c):
        ag_wait(l, c, dd, 0)
        ag_send(l, c, 12, dp_, dd, 0)
        ag_wait(l, c, dd, 1)
        ag_send(l, c, 13, dp_, dd, 1)
        for slot in (dp_, dx + flip, dy + flip, dd + flip):
            for h in (0, 1):
                ag_wait(l, c, slot, h)

    def ln_start():
        for off in range(1, tp):
            cp = rcopy(ln_all.at[me], ln_all.at[me], ln_ss.at[off - 1], ln_rs.at[off - 1], (me + off) % tp)
            cp.start()
            sends.append(cp)

    def ln_finish():
        for off in range(1, tp):
            ref = ln_all.at[(me + tp - off) % tp]
            rcopy(ref, ref, ln_ss.at[off - 1], ln_rs.at[off - 1], dp_).wait_recv()
        for l in range(layers):
            pick = jnp.where(iota2((layers, 128), 0) == l, 1.0, 0.0).astype(BF)
            for s in range(tp):
                ln_col[l, s] = dot(ln_all[s], pick, TN)

    def setup_angles():
        lens = len_row[...].astype(F32)
        for c in range(CHUNKS):
            own = iota2((cr, rows), 1) == iota2((cr, rows), 0) + c * cr
            lc = jnp.sum(jnp.where(own, lens, 0.0), axis=1, keepdims=True)
            len_col[c] = lc
            rep = iota2((hr, rows), 1) == iota2((hr, rows), 0) // heads + c * cr
            len_rep[c] = jnp.sum(jnp.where(rep, lens, 0.0), axis=1, keepdims=True)
            ang = lc * inv_freq[...]
            cos_b[c] = jnp.cos(ang)
            sin_b[c] = jnp.sin(ang)

    def norm_query(l, c):
        cl = pl.ds(c * cw, cw)
        total = jnp.zeros((shard, cw), F32)
        squares = jnp.zeros((shard, cw), F32)
        for s in range(tp):
            v = r_all[l, s, :, cl].astype(F32)
            total = total + v
            squares = squares + v * v
        mean = jnp.sum(total, axis=0, keepdims=True) / width
        var = jnp.sum(squares, axis=0, keepdims=True) / width - mean * mean
        inv = lax.rsqrt(var + NORM_EPS)
        for s in range(tp):
            v = r_all[l, s, :, cl].astype(F32)
            scale = ln_col[l, s]
            scale = jnp.concatenate([scale] * (cw // 128), axis=1)
            h_t[pl.ds(s * shard, shard), cl] = ((v - mean) * inv * scale).astype(BF)
        q_t = dot(w_in_v[l, pl.ds(2 * ffn_dev, q_dev), :], h_t[:, cl])
        q_send[l, cl] = jnp.transpose(q_t).astype(BF)
        for off in range(1, tp):
            dev = (me + off) % tp
            cp = rcopy(q_send.at[l, pl.ds(c * cw + dev * cr, cr)], q_recv.at[l, c, me],
                       q_ss.at[l, c, off - 1], q_rs.at[l, c, off - 1], dev)
            cp.start()
            sends.append(cp)
        q_recv[l, c, me] = q_send[l, pl.ds(pl.multiple_of(c * cw + me * cr, cr), cr)]

    def key_value(l, c):
        per = 128 // cr
        blk = h_t[:, pl.ds(pl.multiple_of(c * cw + (me // per) * 128, 128), 128)]
        here = pl.ds(pl.multiple_of((me % per) * cr, cr), cr)
        kv_tmp[...] = dot(blk, w_key_v[l], TN)
        k = kv_tmp[here].astype(BF).astype(F32)
        x1, x2 = k[:, :half], k[:, half:]
        co, si = cos_b[c], sin_b[c]
        new_k[l, pl.ds(c * cr, cr), :half] = (x1 * co - x2 * si).astype(BF).astype(F32)
        new_k[l, pl.ds(c * cr, cr), half:] = (x2 * co + x1 * si).astype(BF).astype(F32)
        kv_tmp[...] = dot(blk, w_val_v[l], TN)
        new_v[l, pl.ds(c * cr, cr)] = kv_tmp[here].astype(BF).astype(F32)

    def feed_forward(l, c):
        cl = pl.ds(c * cw, cw)
        tile = 288

        def body(i, _):
            o = pl.multiple_of(i * tile, 32)
            gate = dot(w_in_v[l, pl.ds(o, tile)], h_t[:, cl]).astype(BF).astype(F32)
            up = dot(w_in_v[l, pl.ds(o + ffn_dev, tile)], h_t[:, cl]).astype(BF).astype(F32)
            joined[pl.ds(o, tile), cl] = (gate * jax.nn.sigmoid(gate) * up).astype(BF)
            return 0

        lax.fori_loop(0, ffn_dev // tile, body, 0)

    def attention(l, c):
        for off in range(1, tp):
            ref = q_recv.at[l, c, (me + tp - off) % tp]
            rcopy(ref, ref, q_ss.at[l, c, off - 1], q_rs.at[l, c, off - 1], dp_).wait_recv()
        co, si = cos_b[c], sin_b[c]
        r1, r2 = [], []
        for h in range(heads):
            x1 = q_recv[l, c, 2 * h].astype(F32)
            x2 = q_recv[l, c, 2 * h + 1].astype(F32)
            r1.append((x1 * co - x2 * si).astype(BF))
            r2.append((x2 * co + x1 * si).astype(BF))
        ri, ci = iota2((hr, hr), 0), iota2((hr, hr), 1)
        mix = jnp.where(ci == (ri % heads) * cr + ri // heads, 1.0, 0.0).astype(BF)
        q_rows[:, :half] = dot(mix, jnp.concatenate(r1, axis=0)).astype(BF)
        q_rows[:, half:] = dot(mix, jnp.concatenate(r2, axis=0)).astype(BF)
        rep = jnp.where(iota2((hr, cr), 1) == iota2((hr, cr), 0) // heads, 1.0, 0.0).astype(BF)
        k_rep = dot(rep, new_k[l, pl.ds(c * cr, cr)].astype(BF))
        v_rep = dot(rep, new_v[l, pl.ds(c * cr, cr)].astype(BF))
        q_all = q_rows[...].astype(F32)
        s_new = jnp.sum(q_all * k_rep, axis=1, keepdims=True) * head_dim ** -0.5
        group = 16 // heads
        which = iota2((16, head_dim), 0) // heads
        loads[("k", l, c)].wait()

        def score(g, _):
            o = pl.multiple_of(g * 16, 16)
            qg = q_rows[pl.ds(o, 16)]
            acc = jnp.zeros((16, head_dim), F32)
            for j in range(group):
                acc = jnp.where(which == j, dot(qg, k_buf[c * cr + g * group + j], NT), acc)
            s_rows[pl.ds(o, 16)] = acc
            return 0

        lax.fori_loop(0, hr // 16, score, 0, unroll=2)
        s = s_rows[...] * head_dim ** -0.5
        pos = iota2((hr, s.shape[1]), 1).astype(F32)
        s = jnp.where(pos < len_rep[c], s, -1e30)
        top = jnp.maximum(jnp.max(s, axis=1, keepdims=True), s_new)
        w = jnp.exp(s - top)
        w_new = jnp.exp(s_new - top)
        total = jnp.sum(w, axis=1, keepdims=True) + w_new
        q_rows[...] = w.astype(BF)
        loads[("v", l, c)].wait()

        def mixv(g, _):
            o = pl.multiple_of(g * 16, 16)
            wg = q_rows[pl.ds(o, 16)]
            acc = jnp.zeros((16, head_dim), F32)
            for j in range(group):
                acc = jnp.where(which == j, dot(wg, v_buf[c * cr + g * group + j]), acc)
            o_rows[pl.ds(o, 16)] = acc
            return 0

        lax.fori_loop(0, hr // 16, mixv, 0, unroll=2)
        mixed = (o_rows[...] + w_new.astype(BF).astype(F32) * v_rep) / total
        back = jnp.where(ri == (ci % heads) * cr + ci // heads, 1.0, 0.0).astype(BF)
        heads_o = dot(back, mixed.astype(BF)).astype(BF)
        for t in range(tp):
            o_send[l, c, t] = heads_o[(t // 2) * cr:(t // 2 + 1) * cr, (t % 2) * half:(t % 2 + 1) * half]
        for off in range(1, tp):
            dev = (me + off) % tp
            cp = rcopy(o_send.at[l, c, dev], o_recv.at[l, c, me], o_ss.at[l, c, off - 1], o_rs.at[l, c, off - 1], dev)
            cp.start()
            sends.append(cp)
        o_recv[l, c, me] = o_send[l, c, me]

    def project(l, c):
        cl = pl.ds(c * cw, cw)
        for off in range(1, tp):
            ref = o_recv.at[l, c, (me + tp - off) % tp]
            rcopy(ref, ref, o_ss.at[l, c, off - 1], o_rs.at[l, c, off - 1], dp_).wait_recv()
        o_all = jnp.concatenate([o_recv[l, c, j].astype(F32) for j in range(tp)], axis=0)
        joined[pl.ds(ffn_dev, q_dev), cl] = jnp.transpose(o_all).astype(BF)

        def body(i, _):
            o = pl.multiple_of(i * 128, 128)
            y_part[l, pl.ds(o, 128), cl] = dot(w_out_v[l, :, pl.ds(o, 128)], joined[:, cl], TN).astype(BF)
            return 0

        lax.fori_loop(0, width // 128, body, 0)
        for n, slot in enumerate((dd + flip, dx + flip, dy + flip, me + flip)):
            k = slot // 2
            cp = rcopy(y_part.at[l, pl.ds(slot * shard, shard), cl], d2d.at[l, k, :, cl],
                       d_ss.at[l, c, n], d_rs.at[l, c, n], dp_)
            cp.start()
            sends.append(cp)

    def chip_sum(l, c, slot, n, h=None, wait=True):
        k = slot // 2
        cl = pl.ds(c * cw, cw)
        if wait:
            ref = d2d.at[l, k, :, cl]
            rcopy(ref, ref, d_ss.at[l, c, n], d_rs.at[l, c, n], dp_).wait_recv()
        ln = cl if h is None else lanes(c, h)
        mine = y_part[l, pl.ds(pl.multiple_of(slot * shard, 16), shard), ln].astype(F32)
        return mine + d2d[l, k, :, ln].astype(F32)

    def rs_push(l, c, idx, value, dev):
        rs_send[l, c, idx] = value.astype(BF)
        cp = rcopy(rs_send.at[l, c, idx], rs_recv.at[l, c, idx], t_ss.at[l, c, idx], t_rs.at[l, c, idx], dev)
        cp.start()
        sends.append(cp)

    def rs_get(l, c, idx):
        ref = rs_recv.at[l, c, idx]
        rcopy(ref, ref, t_ss.at[l, c, idx], t_rs.at[l, c, idx], dp_).wait_recv()
        return rs_recv[l, c, idx].astype(F32)

    def rs_first(l, c):
        rs_push(l, c, 0, chip_sum(l, c, dd, 0, 0), dx)
        rs_push(l, c, 1, chip_sum(l, c, dd, 0, 1, wait=False), dy)
        rs_push(l, c, 2, chip_sum(l, c, dx, 1, 0), dx)
        rs_push(l, c, 5, chip_sum(l, c, dy, 2, 1), dy)

    def rs_second(l, c):
        rs_push(l, c, 4, chip_sum(l, c, dy, 2, 0, wait=False) + rs_get(l, c, 0), dy)
        rs_push(l, c, 3, chip_sum(l, c, dx, 1, 1, wait=False) + rs_get(l, c, 1), dx)

    def rs_last(l, c):
        first = chip_sum(l, c, me, 3, 0)
        second = chip_sum(l, c, me, 3, 1, wait=False)
        first = first + rs_get(l, c, 2) + rs_get(l, c, 4)
        second = second + rs_get(l, c, 5) + rs_get(l, c, 3)
        a, b = lanes(c, 0), lanes(c, 1)
        return ((r_all[l, me, :, a].astype(F32) + first).astype(BF),
                (r_all[l, me, :, b].astype(F32) + second).astype(BF))

    def keep(l, c, parts):
        r_all[l, me, :, lanes(c, 0)] = parts[0]
        r_all[l, me, :, lanes(c, 1)] = parts[1]
        ag_start(l, c)

    ln_start()
    ag_start(0, 0)
    ag_start(0, 1)
    setup_angles()
    ag_forward(0, 0)
    ag_relay(0, 0)
    ag_forward(0, 1)
    ln_finish()
    ag_finish(0, 0)
    ag_relay(0, 1)
    for l in range(layers):
        loads[("in", l)].wait()
        norm_query(l, 0)
        ag_finish(l, 1)
        loads[("key", l)].wait()
        loads[("val", l)].wait()
        norm_query(l, 1)
        key_value(l, 0)
        key_value(l, 1)
        feed_forward(l, 0)
        if l + 1 < layers:
            load_weights(l + 1)
        attention(l, 0)
        if l + 1 < layers:
            load_cache(l + 1, 0)
        feed_forward(l, 1)
        loads[("out", l)].wait()
        project(l, 0)
        attention(l, 1)
        if l + 1 < layers:
            load_cache(l + 1, 1)
        rs_first(l, 0)
        project(l, 1)
        rs_second(l, 0)
        rs_first(l, 1)
        parts = rs_last(l, 0)
        if l + 1 < layers:
            keep(l + 1, 0, parts)
            rs_second(l, 1)
            ag_forward(l + 1, 0)
            keep(l + 1, 1, rs_last(l, 1))
            ag_relay(l + 1, 0)
            ag_forward(l + 1, 1)
            ag_finish(l + 1, 0)
            ag_relay(l + 1, 1)
        else:
            rs_second(l, 1)
            full = jnp.concatenate(parts + rs_last(l, 1), axis=1)
            r_out[...] = dot(full, perm[...], NT).astype(BF)
    for cp in sends:
        cp.wait_send()


def cache_kernel(lengths, new_k, new_v, k_cache, v_cache, k_out, v_out, ring, in_sems, out_sems):
    layers, rows = k_cache.shape[:2]
    depth, per = ring.shape[0], ring.shape[1]
    groups = rows // per
    jobs = []
    for l in range(layers):
        for g in range(groups):
            jobs.append((k_cache, k_out, new_k, l, g))
            jobs.append((v_cache, v_out, new_v, l, g))
    n = len(jobs)
    ahead = depth - 6

    def fetch(i):
        src, _, _, l, g = jobs[i]
        return pltpu.make_async_copy(src.at[l, pl.ds(g * per, per)], ring.at[i % depth], in_sems.at[i % depth])

    def put(i):
        _, dst, _, l, g = jobs[i]
        return pltpu.make_async_copy(ring.at[i % depth], dst.at[l, pl.ds(g * per, per)], out_sems.at[i % depth])

    for i in range(ahead):
        fetch(i).start()
    for i in range(n):
        fetch(i).wait()
        _, _, new, l, g = jobs[i]
        fresh = new[l, pl.ds(g * per, per)]
        for b in range(per):
            slot = lengths[g * per + b]
            base = pl.multiple_of((slot // 16) * 16, 16)
            old = ring[i % depth, b, pl.ds(base, 16)].astype(F32)
            hit = iota2(old.shape, 0) == slot - base
            ring[i % depth, b, pl.ds(base, 16)] = jnp.where(hit, fresh[b:b + 1], old).astype(BF)
        put(i).start()
        nxt = i + ahead
        if nxt < n:
            if nxt >= depth:
                put(nxt - depth).wait()
            fetch(nxt).start()
    for i in range(max(0, n - depth), n):
        put(i).wait()


def solution(mesh):
    tp = mesh.shape["tp"]

    def device_step(residual, lengths, ln_scale, w_in, w_key, w_val, w_out, key_cache, val_cache):
        layers, width, in_cols = w_in.shape
        batch, shard = residual.shape
        rows = lengths.shape[0]
        head_dim = w_key.shape[2]
        ffn_dev = in_cols - w_out.shape[1]
        q_dev = w_out.shape[1] - ffn_dev
        heads = q_dev * tp // head_dim
        cw, cr = batch // CHUNKS, rows // CHUNKS
        hr = cr * heads
        slots = key_cache.shape[2]
        inv_freq = jnp.asarray((10000.0 ** (-np.arange(head_dim // 2) * (2.0 / head_dim))).astype(np.float32))[None, :]
        vmem = pl.BlockSpec(memory_space=pltpu.VMEM)
        hbm = pl.BlockSpec(memory_space=pltpu.HBM)
        smem = pl.BlockSpec(memory_space=pltpu.SMEM)
        dma = pltpu.SemaphoreType.DMA
        r_new, new_k, new_v = pl.pallas_call(
            step_kernel,
            out_shape=[jax.ShapeDtypeStruct((shard, batch), BF),
                       jax.ShapeDtypeStruct((layers, rows, head_dim), F32),
                       jax.ShapeDtypeStruct((layers, rows, head_dim), F32)],
            in_specs=[vmem] * 4 + [hbm] * 6,
            out_specs=[vmem] * 3,
            scratch_shapes=[
                pltpu.VMEM((layers, in_cols, width), BF),
                pltpu.VMEM((layers, width, head_dim), BF),
                pltpu.VMEM((layers, width, head_dim), BF),
                pltpu.VMEM((layers, w_out.shape[1], width), BF),
                pltpu.VMEM((rows, slots, head_dim), BF),
                pltpu.VMEM((rows, slots, head_dim), BF),
                pltpu.VMEM((layers, tp, shard, batch), BF),
                pltpu.VMEM((tp, layers, shard), BF),
                pltpu.VMEM((layers, tp, shard, 128), F32),
                pltpu.VMEM((width, batch), BF),
                pltpu.VMEM((ffn_dev + q_dev, batch), BF),
                pltpu.VMEM((layers, width, batch), BF),
                pltpu.VMEM((layers, tp // 2, shard, batch), BF),
                pltpu.VMEM((layers, CHUNKS, 6, shard, cw // 2), BF),
                pltpu.VMEM((layers, CHUNKS, 6, shard, cw // 2), BF),
                pltpu.VMEM((layers, batch, q_dev), BF),
                pltpu.VMEM((layers, CHUNKS, tp, cr, q_dev), BF),
                pltpu.VMEM((layers, CHUNKS, tp, cr, q_dev), BF),
                pltpu.VMEM((layers, CHUNKS, tp, cr, q_dev), BF),
                pltpu.VMEM((hr, head_dim), BF),
                pltpu.VMEM((hr, slots), F32),
                pltpu.VMEM((hr, head_dim), F32),
                pltpu.VMEM((128, head_dim), F32),
                pltpu.VMEM((CHUNKS, cr, head_dim // 2), F32),
                pltpu.VMEM((CHUNKS, cr, head_dim // 2), F32),
                pltpu.VMEM((CHUNKS, cr, 1), F32),
                pltpu.VMEM((CHUNKS, hr, 1), F32),
                pltpu.VMEM((batch, batch), BF),
                dma((layers, 4)), dma((layers, CHUNKS, 2)),
                dma((tp - 1,)), dma((tp - 1,)),
                dma((layers, CHUNKS, 14)), dma((layers, CHUNKS, tp, 2)),
                dma((layers, CHUNKS, tp - 1)), dma((layers, CHUNKS, tp - 1)),
                dma((layers, CHUNKS, tp - 1)), dma((layers, CHUNKS, tp - 1)),
                dma((layers, CHUNKS, 4)), dma((layers, CHUNKS, 4)),
                dma((layers, CHUNKS, 6)), dma((layers, CHUNKS, 6)),
            ],
            compiler_params=pltpu.CompilerParams(collective_id=0, has_side_effects=True, vmem_limit_bytes=60 * 2 ** 20),
            name="step",
        )(residual.T, lengths[None, :], ln_scale, inv_freq, jnp.swapaxes(w_in, 1, 2), w_key, w_val, w_out, key_cache, val_cache)
        key_out, val_out = pl.pallas_call(
            cache_kernel,
            out_shape=[jax.ShapeDtypeStruct(key_cache.shape, BF)] * 2,
            in_specs=[smem, vmem, vmem, hbm, hbm],
            out_specs=[hbm, hbm],
            scratch_shapes=[pltpu.VMEM((20, 8, slots, head_dim), BF), dma((20,)), dma((20,))],
            compiler_params=pltpu.CompilerParams(vmem_limit_bytes=40 * 2 ** 20),
            name="caches",
        )(lengths, new_k, new_v, key_cache, val_cache)
        return r_new.T, key_out, val_out

    cache_spec = P(None, ("dp", "tp"), None, None)
    return jax.shard_map(device_step, mesh=mesh, in_specs=(P("dp", "tp"), P(("dp", "tp")), P(None, "tp"), P(None, None, "tp"), P(), P(), P(None, "tp", None), cache_spec, cache_spec), out_specs=(P("dp", "tp"), cache_spec, cache_spec), check_vma=False)
```

time: 239 us -> 110 us (0.46)
  Pallas kernels: 0 us -> 106 us
  waiting for transfers between devices: 80.8 us -> 0 us
  blocking collectives: 47.5 us -> 0 us
  matrix products: 46.4 us -> 0 us
  other arithmetic: 36.9 us -> 0 us
  between operations: 14.2 us -> 0.68 us
  starting transfers between devices: 8.59 us -> 0 us
    pallas_call x0 -> x2, Pallas kernels: none -> 106 us  [the longest x1 82.9 us: device_step(): pl.pallas_call(step_kernel, out_shape=[jax.ShapeDtypeStruct((shard, batch...]
    psum x2 -> x0, blocking collectives: 47.5 us -> none  [norm_sharded(): row_stats = lax.psum(row_stats, 'tp')]
    dot_general x14 -> x0, matrix products: 46.4 us -> none  [the longest x2 11.5 us: attend(): jnp.einsum('bhd,bsd->bhs', query_rows, key_cache, preferred_element_type=...]
    all_gather x2 -> x0, waiting for transfers between devices: 37 us -> none  [device_step(): normed = lax.all_gather(normed_local, 'tp', axis=1, tiled=True)]
    reduce_scatter x2 -> x0, waiting for transfers between devices: 31.9 us -> none  [device_step(): lax.psum_scatter(partial_sum, 'tp', scatter_dimension=1, tiled=True)]
    select_n x1 -> x0, other arithmetic: 23 us -> none  [device_step(): jnp.where(slot_mask, jnp.stack(new_vals)[:, :, None, :], val_cache)]
    all_to_all x4 -> x0, waiting for transfers between devices: 11.8 us -> none  [the longest x2 8.83 us: device_step(): lax.all_to_all(attn_rows.reshape(rows_dev, num_heads * head_dim), 'tp', 1...]
    all_to_all x4 -> x0, starting transfers between devices: 8.42 us -> none  [the longest x2 4.21 us: device_step(): lax.all_to_all(attn_rows.reshape(rows_dev, num_heads * head_dim), 'tp', 1...]
  transfers between devices with their start and end apart: 8 -> 0, of which waited for: 8 -> 0; matrix products, arithmetic and copies ran while one was open for 14% -> 0% of each run, Pallas kernels for 0% -> 0%
where the time goes in v1:
time: 110 us; the launch traced here: 109 us
  Pallas kernels  106 us (96%)
  local copies, waits for them, and re-layouts  2.47 us (2%)
    pallas_call x1, Pallas kernels, device_step(): pl.pallas_call(step_kernel, out_shape=[jax.ShapeDtypeStruct((shard, batch...  82.9 us
    pallas_call x1, Pallas kernels, device_step(): pl.pallas_call(cache_kernel, out_shape=[jax.ShapeDtypeStruct(key_cache.sh...  23.4 us
    unnamed x9, local copies, waits for them, and re-layouts  2.47 us

profile of v1, /device:TPU:0, one launch (start us, length us, event | category | flops | bytes accessed | tf_op | source)
XLA Modules:
  0.0 109.4 jit_solution(3361817554745404812)
XLA Ops:
  0.6 0.0 copy-start.2
  0.6 82.9 %step.1 = (bf16[144,512]{1,0:T(8,128)(2,1)}, f32[2,64,256]{2,1,0:T(8,128)}, f32[2,64,256]{2,1,0:T(8,128)}) custom-call(bf16[144,512]{1,0:T(8,128)(2,1)} %bitcast.6, s32[1,64]{1,0:T(1,128)} %bitcast.4, bf16[2,144]{1,0:T(2,128)(2,1)} %ln_in.1, f32[1,128]{1,0:T(1,128)} %constant.3.inv_freq, bf16[2,1856,1152]{2,1,0:T(8,128)(2,1)} %bitcast.5, ...), custom_call_target="tpu_custom_call" | custom-call | tf_op jit(solution)/shard_map/step/pallas_call | solution.py:467
  83.5 0.0 copy-done.2
  83.5 0.0 copy-start
  83.6 0.9 copy-done
  84.4 0.0 copy-start.1
  84.4 0.9 copy-done.1
  85.4 0.0 copy-start.3
  85.4 23.4 %caches.1 = (bf16[2,64,256,256]{3,2,1,0:T(8,128)(2,1)}, bf16[2,64,256,256]{3,2,1,0:T(8,128)(2,1)}) custom-call(s32[64]{0:T(128)S(1)} %copy-done.2, f32[2,64,256]{2,1,0:T(8,128)S(1)} %copy-done, f32[2,64,256]{2,1,0:T(8,128)S(1)} %copy-done.1, bf16[2,64,256,256]{3,2,1,0:T(8,128)(2,1)} %k_cache.3, bf16[2,64,256,256]{3,2,1,0:T(8,128)(2,1)} %v_cache.3), custom_call_target="tpu_custom_call" | custom-call | tf_op jit(solution)/shard_map/caches/pallas_call | solution.py:514
  108.8 0.0 copy-done.3
  108.8 0.7 copy.14
Async XLA Ops:
  0.6 82.9 %copy-start.2 = (s32[64]{0:T(128)S(1)}, s32[64]{0:T(128)}, u32[]{:S(2)}) copy-start(s32[64]{0:T(128)} %lengths.1) | copy-start | bytes 772
  83.5 0.9 copy-start
  84.4 0.9 copy-start.1
  85.4 23.4 %copy-start.3 = (bf16[144,512]{1,0:T(8,128)(2,1)S(1)}, bf16[144,512]{1,0:T(8,128)(2,1)}, u32[]{:S(2)}) copy-start(bf16[144,512]{1,0:T(8,128)(2,1)} %get-tuple-element.8) | copy-start | bytes 442372

commit v2 on v1

v2 whole, which is shorter than its diff:
```python
import functools

import jax
import jax.numpy as jnp
import numpy as np
from jax import lax
from jax.experimental import pallas as pl
from jax.experimental.pallas import tpu as pltpu
from jax.sharding import PartitionSpec as P

NORM_EPS = 1e-6
MESH = pl.DeviceIdType.MESH
CHUNKS = 2
BF = jnp.bfloat16
F32 = jnp.float32
TN = (((0,), (0,)), ((), ()))
NT = (((1,), (1,)), ((), ()))


def dot(a, b, dims=None):
    if dims is None:
        return jnp.dot(a, b, preferred_element_type=F32)
    return lax.dot_general(a, b, dims, preferred_element_type=F32)


def iota2(shape, dim):
    return lax.broadcasted_iota(jnp.int32, shape, dim)


def step_kernel(r_in, len_row, ln_in, inv_freq, w_in, w_key, w_val, w_out, k_cache, v_cache,
                r_out, new_k, new_v, kv_all,
                w_in_v, w_key_v, w_val_v, w_out_v, w_out_t,
                r_all, ln_all, ln_col, h_t, joined, y_part, d2d, rs_recv, rs_send,
                q_send, q_recv, o_send, o_recv, q_rows, s_rows, o_rows, kv_tmp,
                cos_b, sin_b, len_col, len_rep, perm,
                w_sems, c_sems, ln_ss, ln_rs, ag_ss, ag_rs, q_ss, q_rs, o_ss, o_rs, d_ss, d_rs, t_ss, t_rs):
    layers, width = w_in.shape[0], w_in.shape[2]
    shard, batch = r_in.shape
    tp = width // shard
    rows = batch // tp
    q_dev = q_send.shape[2]
    ffn_dev = w_out.shape[1] - q_dev
    head_dim = w_key.shape[2]
    half = head_dim // 2
    heads = q_dev * tp // head_dim
    cw = batch // CHUNKS
    cr = rows // CHUNKS
    hr = cr * heads

    me = lax.axis_index("tp")
    core, xpos, ypos = me % 2, (me // 2) % 2, me // 4
    dp_ = me + 1 - 2 * core
    dx = me + 2 - 4 * xpos
    dy = me + 4 - 8 * ypos
    dd = dx + 4 - 8 * ypos
    flip = 1 - 2 * core

    def rcopy(src, dst, ss, rs, dev):
        return pltpu.make_async_remote_copy(src_ref=src, dst_ref=dst, send_sem=ss, recv_sem=rs,
                                            device_id={"tp": dev}, device_id_type=MESH)

    barrier = pltpu.get_barrier_semaphore()
    for off in range(1, tp):
        pl.semaphore_signal(barrier, 1, device_id={"tp": (me + off) % tp}, device_id_type=MESH)

    loads = {}

    def load(name, src, dst, sem):
        loads[name] = pltpu.make_async_copy(src, dst, sem)
        loads[name].start()

    def load_in(l):
        load(("key", l), w_key.at[l], w_key_v, w_sems.at[l, 1])
        load(("val", l), w_val.at[l], w_val_v, w_sems.at[l, 2])
        load(("in", l), w_in.at[l], w_in_v, w_sems.at[l, 0])

    def load_out(l):
        load(("out", l), w_out.at[l], w_out_v, w_sems.at[l, 3])

    def load_cache(l):
        load(("k", l), k_cache.at[l], kv_all.at[0, l], c_sems.at[l, 0])
        load(("v", l), v_cache.at[l], kv_all.at[1, l], c_sems.at[l, 1])

    load_out(0)
    load_in(0)
    load_cache(0)

    src_i = iota2((batch, batch), 0)
    dst_i = iota2((batch, batch), 1)
    want = ((dst_i % cw) // cr) * rows + (dst_i // cw) * cr + dst_i % cr
    perm[...] = jnp.where(src_i == want, 1.0, 0.0).astype(BF)
    r_all[0, me] = dot(r_in[...], perm[...]).astype(BF)
    ln_all[me] = ln_in[...]

    pl.semaphore_wait(barrier, tp - 1)

    sends = []

    def lanes(c):
        return pl.ds(c * cw, cw)

    def ag_send(l, c, idx, dev, slot):
        ref = r_all.at[l, slot, :, lanes(c)]
        cp = rcopy(ref, ref, ag_ss.at[l, c, idx], ag_rs.at[l, c, slot], dev)
        cp.start()
        sends.append(cp)

    def ag_wait(l, c, slot):
        ref = r_all.at[l, slot, :, lanes(c)]
        rcopy(ref, ref, ag_ss.at[l, c, 0], ag_rs.at[l, c, slot], dp_).wait_recv()

    def ag_start(l, c):
        ag_send(l, c, 0, dd, me)
        ag_send(l, c, 1, dx, me)
        ag_send(l, c, 2, dy, me)
        ag_send(l, c, 3, dp_, me)

    def ag_relay(l, c):
        for n, slot in enumerate((dx, dy, dd)):
            ag_wait(l, c, slot)
            ag_send(l, c, 4 + n, dp_, slot)

    def ag_finish(l, c):
        for slot in (dp_, dx + flip, dy + flip, dd + flip):
            ag_wait(l, c, slot)

    def ln_start():
        for off in range(1, tp):
            cp = rcopy(ln_all.at[me], ln_all.at[me], ln_ss.at[off - 1], ln_rs.at[off - 1], (me + off) % tp)
            cp.start()
            sends.append(cp)

    def ln_finish():
        for off in range(1, tp):
            ref = ln_all.at[(me + tp - off) % tp]
            rcopy(ref, ref, ln_ss.at[off - 1], ln_rs.at[off - 1], dp_).wait_recv()
        for l in range(layers):
            pick = jnp.where(iota2((layers, 128), 0) == l, 1.0, 0.0).astype(BF)
            for s in range(tp):
                ln_col[l, s] = dot(ln_all[s], pick, TN)

    def setup_angles():
        lens = len_row[...].astype(F32)
        for c in range(CHUNKS):
            own = iota2((cr, rows), 1) == iota2((cr, rows), 0) + c * cr
            lc = jnp.sum(jnp.where(own, lens, 0.0), axis=1, keepdims=True)
            len_col[c] = lc
            rep = iota2((hr, rows), 1) == iota2((hr, rows), 0) // heads + c * cr
            len_rep[c] = jnp.sum(jnp.where(rep, lens, 0.0), axis=1, keepdims=True)
            ang = lc * inv_freq[...]
            cos_b[c] = jnp.cos(ang)
            sin_b[c] = jnp.sin(ang)

    def norm_query(l, c):
        cl = pl.ds(c * cw, cw)
        total = jnp.zeros((shard, cw), F32)
        squares = jnp.zeros((shard, cw), F32)
        for s in range(tp):
            v = r_all[l, s, :, cl].astype(F32)
            total = total + v
            squares = squares + v * v
        mean = jnp.sum(total, axis=0, keepdims=True) / width
        var = jnp.sum(squares, axis=0, keepdims=True) / width - mean * mean
        inv = lax.rsqrt(var + NORM_EPS)
        for s in range(tp):
            v = r_all[l, s, :, cl].astype(F32)
            scale = ln_col[l, s]
            scale = jnp.concatenate([scale] * (cw // 128), axis=1)
            h_t[pl.ds(s * shard, shard), cl] = ((v - mean) * inv * scale).astype(BF)
        q_t = dot(w_in_v[pl.ds(2 * ffn_dev, q_dev), :], h_t[:, cl])
        q_send[l, cl] = jnp.transpose(q_t).astype(BF)
        for off in range(1, tp):
            dev = (me + off) % tp
            cp = rcopy(q_send.at[l, pl.ds(c * cw + dev * cr, cr)], q_recv.at[l, c, me],
                       q_ss.at[l, c, off - 1], q_rs.at[l, c, off - 1], dev)
            cp.start()
            sends.append(cp)
        q_recv[l, c, me] = q_send[l, pl.ds(pl.multiple_of(c * cw + me * cr, cr), cr)]

    def key_value(l, c):
        per = 128 // cr
        blk = h_t[:, pl.ds(pl.multiple_of(c * cw + (me // per) * 128, 128), 128)]
        here = pl.ds(pl.multiple_of((me % per) * cr, cr), cr)
        kv_tmp[...] = dot(blk, w_key_v[...], TN)
        k = kv_tmp[here].astype(BF).astype(F32)
        x1, x2 = k[:, :half], k[:, half:]
        co, si = cos_b[c], sin_b[c]
        new_k[l, pl.ds(c * cr, cr), :half] = (x1 * co - x2 * si).astype(BF).astype(F32)
        new_k[l, pl.ds(c * cr, cr), half:] = (x2 * co + x1 * si).astype(BF).astype(F32)
        kv_tmp[...] = dot(blk, w_val_v[...], TN)
        new_v[l, pl.ds(c * cr, cr)] = kv_tmp[here].astype(BF).astype(F32)

    def feed_forward(l, c):
        cl = pl.ds(c * cw, cw)
        tile = 288

        def body(i, _):
            o = pl.multiple_of(i * tile, 32)
            gate = dot(w_in_v[pl.ds(o, tile)], h_t[:, cl]).astype(BF).astype(F32)
            up = dot(w_in_v[pl.ds(o + ffn_dev, tile)], h_t[:, cl]).astype(BF).astype(F32)
            joined[pl.ds(o, tile), cl] = (gate * jax.nn.sigmoid(gate) * up).astype(BF)
            return 0

        lax.fori_loop(0, ffn_dev // tile, body, 0)

    def attention(l, c):
        for off in range(1, tp):
            ref = q_recv.at[l, c, (me + tp - off) % tp]
            rcopy(ref, ref, q_ss.at[l, c, off - 1], q_rs.at[l, c, off - 1], dp_).wait_recv()
        co, si = cos_b[c], sin_b[c]
        r1, r2 = [], []
        for h in range(heads):
            x1 = q_recv[l, c, 2 * h].astype(F32)
            x2 = q_recv[l, c, 2 * h + 1].astype(F32)
            r1.append((x1 * co - x2 * si).astype(BF))
            r2.append((x2 * co + x1 * si).astype(BF))
        ri, ci = iota2((hr, hr), 0), iota2((hr, hr), 1)
        mix = jnp.where(ci == (ri % heads) * cr + ri // heads, 1.0, 0.0).astype(BF)
        q_rows[:, :half] = dot(mix, jnp.concatenate(r1, axis=0)).astype(BF)
        q_rows[:, half:] = dot(mix, jnp.concatenate(r2, axis=0)).astype(BF)
        rep = jnp.where(iota2((hr, cr), 1) == iota2((hr, cr), 0) // heads, 1.0, 0.0).astype(BF)
        k_rep = dot(rep, new_k[l, pl.ds(c * cr, cr)].astype(BF))
        v_rep = dot(rep, new_v[l, pl.ds(c * cr, cr)].astype(BF))
        q_all = q_rows[...].astype(F32)
        s_new = jnp.sum(q_all * k_rep, axis=1, keepdims=True) * head_dim ** -0.5
        group = 16 // heads
        which = iota2((16, head_dim), 0) // heads
        if c == 0:
            loads[("k", l)].wait()

        def score(g, _):
            o = pl.multiple_of(g * 16, 16)
            qg = q_rows[pl.ds(o, 16)]
            acc = jnp.zeros((16, head_dim), F32)
            for j in range(group):
                acc = jnp.where(which == j, dot(qg, kv_all[0, l, c * cr + g * group + j], NT), acc)
            s_rows[pl.ds(o, 16)] = acc
            return 0

        lax.fori_loop(0, hr // 16, score, 0, unroll=4)
        s = s_rows[...] * head_dim ** -0.5
        pos = iota2((hr, s.shape[1]), 1).astype(F32)
        s = jnp.where(pos < len_rep[c], s, -1e30)
        top = jnp.maximum(jnp.max(s, axis=1, keepdims=True), s_new)
        w = jnp.exp(s - top)
        w_new = jnp.exp(s_new - top)
        total = jnp.sum(w, axis=1, keepdims=True) + w_new
        q_rows[...] = w.astype(BF)
        if c == 0:
            loads[("v", l)].wait()

        def mixv(g, _):
            o = pl.multiple_of(g * 16, 16)
            wg = q_rows[pl.ds(o, 16)]
            acc = jnp.zeros((16, head_dim), F32)
            for j in range(group):
                acc = jnp.where(which == j, dot(wg, kv_all[1, l, c * cr + g * group + j]), acc)
            o_rows[pl.ds(o, 16)] = acc
            return 0

        lax.fori_loop(0, hr // 16, mixv, 0, unroll=4)
        mixed = (o_rows[...] + w_new.astype(BF).astype(F32) * v_rep) / total
        back = jnp.where(ri == (ci % heads) * cr + ci // heads, 1.0, 0.0).astype(BF)
        heads_o = dot(back, mixed.astype(BF)).astype(BF)
        for t in range(tp):
            o_send[l, c, t] = heads_o[(t // 2) * cr:(t // 2 + 1) * cr, (t % 2) * half:(t % 2 + 1) * half]
        for off in range(1, tp):
            dev = (me + off) % tp
            cp = rcopy(o_send.at[l, c, dev], o_recv.at[l, c, me], o_ss.at[l, c, off - 1], o_rs.at[l, c, off - 1], dev)
            cp.start()
            sends.append(cp)
        o_recv[l, c, me] = o_send[l, c, me]

    def project(l, c):
        cl = pl.ds(c * cw, cw)
        for off in range(1, tp):
            ref = o_recv.at[l, c, (me + tp - off) % tp]
            rcopy(ref, ref, o_ss.at[l, c, off - 1], o_rs.at[l, c, off - 1], dp_).wait_recv()
        o_all = jnp.concatenate([o_recv[l, c, j].astype(F32) for j in range(tp)], axis=0)
        joined[pl.ds(ffn_dev, q_dev), cl] = jnp.transpose(o_all).astype(BF)

        for n, slot in enumerate((dd + flip, dx + flip, dy + flip, me + flip, dd, dx, dy, me)):
            at = pl.ds(pl.multiple_of(slot * shard, 16), shard)
            y_part[l, at, cl] = dot(w_out_t[at], joined[:, cl]).astype(BF)
            if n < 4:
                cp = rcopy(y_part.at[l, at, cl], d2d.at[l, slot // 2, :, cl], d_ss.at[l, c, n], d_rs.at[l, c, n], dp_)
                cp.start()
                sends.append(cp)

    def turn_out(l):
        loads[("out", l)].wait()

        def body(i, _):
            o = pl.multiple_of(i * 128, 128)
            w_out_t[pl.ds(o, 128)] = jnp.transpose(w_out_v[:, pl.ds(o, 128)])
            return 0

        lax.fori_loop(0, width // 128, body, 0)

    def chip_sum(l, c, slot, n):
        ref = d2d.at[l, slot // 2, :, lanes(c)]
        rcopy(ref, ref, d_ss.at[l, c, n], d_rs.at[l, c, n], dp_).wait_recv()
        mine = y_part[l, pl.ds(pl.multiple_of(slot * shard, 16), shard), lanes(c)].astype(F32)
        return mine + d2d[l, slot // 2, :, lanes(c)].astype(F32)

    def rs_first(l, c):
        for n, dev in enumerate((dd, dx, dy)):
            rs_send[l, c, n] = chip_sum(l, c, dev, n).astype(BF)
            cp = rcopy(rs_send.at[l, c, n], rs_recv.at[l, c, n], t_ss.at[l, c, n], t_rs.at[l, c, n], dev)
            cp.start()
            sends.append(cp)

    def rs_last(l, c):
        total = chip_sum(l, c, me, 3)
        for n in (1, 2, 0):
            ref = rs_recv.at[l, c, n]
            rcopy(ref, ref, t_ss.at[l, c, n], t_rs.at[l, c, n], dp_).wait_recv()
            total = total + rs_recv[l, c, n].astype(F32)
        return (r_all[l, me, :, lanes(c)].astype(F32) + total).astype(BF)

    def keep(l, c, part):
        r_all[l, me, :, lanes(c)] = part
        ag_start(l, c)

    ln_start()
    ag_start(0, 0)
    ag_start(0, 1)
    setup_angles()
    turn_out(0)
    ag_relay(0, 0)
    ln_finish()
    ag_finish(0, 0)
    for l in range(layers):
        loads[("in", l)].wait()
        norm_query(l, 0)
        load_cache(l + 1) if l + 1 < layers else None
        ag_relay(l, 1)
        ag_finish(l, 1)
        norm_query(l, 1)
        loads[("key", l)].wait()
        loads[("val", l)].wait()
        key_value(l, 0)
        key_value(l, 1)
        feed_forward(l, 0)
        attention(l, 0)
        attention(l, 1)
        feed_forward(l, 1)
        if l + 1 < layers:
            load_in(l + 1)
            load_out(l + 1)
        project(l, 0)
        project(l, 1)
        rs_first(l, 0)
        rs_first(l, 1)
        if l + 1 < layers:
            turn_out(l + 1)
            keep(l + 1, 0, rs_last(l, 0))
            keep(l + 1, 1, rs_last(l, 1))
            ag_relay(l + 1, 0)
            ag_finish(l + 1, 0)
        else:
            full = jnp.concatenate([rs_last(l, 0), rs_last(l, 1)], axis=1)
            r_out[...] = dot(full, perm[...], NT).astype(BF)
    for cp in sends:
        cp.wait_send()


def cache_kernel(lengths, new_k, new_v, kv_all, k_out, v_out, tiles, big_sems, tile_sems):
    layers, rows = kv_all.shape[1:3]
    per = 16
    pairs = [(kv_all.at[0], k_out, new_k, 0), (kv_all.at[1], v_out, new_v, 1)]
    jobs = [(l, g, pair) for l in range(layers) for pair in pairs for g in range(rows // per)]

    def big(i):
        l, g, (src, dst, _, _) = jobs[i]
        at = pl.ds(g * per, per)
        return pltpu.make_async_copy(src.at[l, at], dst.at[l, at], big_sems.at[i])

    for i in range(len(jobs)):
        big(i).start()

    def build(b, _):
        slot = lengths[b]
        base = pl.multiple_of((slot // 16) * 16, 16)
        hit = iota2((16, kv_all.shape[4]), 0) == slot - base
        for l in range(layers):
            for src, _, new, n in pairs:
                old = src[l, b, pl.ds(base, 16)].astype(F32)
                tiles[l, n, b] = jnp.where(hit, new[l, pl.ds(b, 1)], old).astype(BF)
        return 0

    lax.fori_loop(0, rows, build, 0, unroll=4)
    for i in range(len(jobs)):
        l, g, (_, dst, _, n) = jobs[i]
        big(i).wait()

        def patch(j, _):
            b = g * per + j
            base = pl.multiple_of((lengths[b] // 16) * 16, 16)
            pltpu.make_async_copy(tiles.at[l, n, b], dst.at[l, b, pl.ds(base, 16)], tile_sems.at[i]).start()
            return 0

        lax.fori_loop(0, per, patch, 0, unroll=4)
    for i in range(len(jobs)):
        l, g, (_, dst, _, n) = jobs[i]
        at = pl.ds(g * per, per)
        pltpu.make_async_copy(tiles.at[l, n, at], dst.at[l, at, pl.ds(0, 16)], tile_sems.at[i]).wait()


def solution(mesh):
    tp = mesh.shape["tp"]

    def device_step(residual, lengths, ln_scale, w_in, w_key, w_val, w_out, key_cache, val_cache):
        layers, width, in_cols = w_in.shape
        batch, shard = residual.shape
        rows = lengths.shape[0]
        head_dim = w_key.shape[2]
        ffn_dev = in_cols - w_out.shape[1]
        q_dev = w_out.shape[1] - ffn_dev
        heads = q_dev * tp // head_dim
        cw, cr = batch // CHUNKS, rows // CHUNKS
        hr = cr * heads
        slots = key_cache.shape[2]
        inv_freq = jnp.asarray((10000.0 ** (-np.arange(head_dim // 2) * (2.0 / head_dim))).astype(np.float32))[None, :]
        vmem = pl.BlockSpec(memory_space=pltpu.VMEM)
        hbm = pl.BlockSpec(memory_space=pltpu.HBM)
        smem = pl.BlockSpec(memory_space=pltpu.SMEM)
        dma = pltpu.SemaphoreType.DMA
        r_new, new_k, new_v, kv_all = pl.pallas_call(
            step_kernel,
            out_shape=[jax.ShapeDtypeStruct((shard, batch), BF),
                       pltpu.VMEM((layers, rows, head_dim), F32),
                       pltpu.VMEM((layers, rows, head_dim), F32),
                       pltpu.VMEM((2,) + key_cache.shape, BF)],
            in_specs=[vmem] * 4 + [hbm] * 6,
            out_specs=[vmem] * 4,
            scratch_shapes=[
                pltpu.VMEM((in_cols, width), BF),
                pltpu.VMEM((width, head_dim), BF),
                pltpu.VMEM((width, head_dim), BF),
                pltpu.VMEM((w_out.shape[1], width), BF),
                pltpu.VMEM((width, w_out.shape[1]), BF),
                pltpu.VMEM((layers, tp, shard, batch), BF),
                pltpu.VMEM((tp, layers, shard), BF),
                pltpu.VMEM((layers, tp, shard, 128), F32),
                pltpu.VMEM((width, batch), BF),
                pltpu.VMEM((ffn_dev + q_dev, batch), BF),
                pltpu.VMEM((layers, width, batch), BF),
                pltpu.VMEM((layers, tp // 2, shard, batch), BF),
                pltpu.VMEM((layers, CHUNKS, 3, shard, cw), BF),
                pltpu.VMEM((layers, CHUNKS, 3, shard, cw), BF),
                pltpu.VMEM((layers, batch, q_dev), BF),
                pltpu.VMEM((layers, CHUNKS, tp, cr, q_dev), BF),
                pltpu.VMEM((layers, CHUNKS, tp, cr, q_dev), BF),
                pltpu.VMEM((layers, CHUNKS, tp, cr, q_dev), BF),
                pltpu.VMEM((hr, head_dim), BF),
                pltpu.VMEM((hr, slots), F32),
                pltpu.VMEM((hr, head_dim), F32),
                pltpu.VMEM((128, head_dim), F32),
                pltpu.VMEM((CHUNKS, cr, head_dim // 2), F32),
                pltpu.VMEM((CHUNKS, cr, head_dim // 2), F32),
                pltpu.VMEM((CHUNKS, cr, 1), F32),
                pltpu.VMEM((CHUNKS, hr, 1), F32),
                pltpu.VMEM((batch, batch), BF),
                dma((layers, 4)), dma((layers, 2)),
                dma((tp - 1,)), dma((tp - 1,)),
                dma((layers, CHUNKS, 7)), dma((layers, CHUNKS, tp)),
                dma((layers, CHUNKS, tp - 1)), dma((layers, CHUNKS, tp - 1)),
                dma((layers, CHUNKS, tp - 1)), dma((layers, CHUNKS, tp - 1)),
                dma((layers, CHUNKS, 4)), dma((layers, CHUNKS, 4)),
                dma((layers, CHUNKS, 3)), dma((layers, CHUNKS, 3)),
            ],
            compiler_params=pltpu.CompilerParams(collective_id=0, has_side_effects=True, vmem_limit_bytes=27 * 2 ** 20),
            name="step",
        )(residual.T, lengths[None, :], ln_scale, inv_freq, jnp.swapaxes(w_in, 1, 2), w_key, w_val, w_out, key_cache, val_cache)
        keep = functools.partial(pltpu.with_memory_space_constraint, memory_space=pltpu.VMEM)
        key_out, val_out = pl.pallas_call(
            cache_kernel,
            out_shape=[jax.ShapeDtypeStruct(key_cache.shape, BF)] * 2,
            in_specs=[smem] + [vmem] * 3,
            out_specs=[hbm, hbm],
            scratch_shapes=[pltpu.VMEM((layers, 2, rows, 16, head_dim), BF), dma((16,)), dma((16,))],
            compiler_params=pltpu.CompilerParams(vmem_limit_bytes=5 * 2 ** 20),
            name="caches",
        )(lengths, keep(new_k), keep(new_v), keep(kv_all))
        return r_new.T, key_out, val_out

    cache_spec = P(None, ("dp", "tp"), None, None)
    return jax.shard_map(device_step, mesh=mesh, in_specs=(P("dp", "tp"), P(("dp", "tp")), P(None, "tp"), P(None, None, "tp"), P(), P(), P(None, "tp", None), cache_spec, cache_spec), out_specs=(P("dp", "tp"), cache_spec, cache_spec), check_vma=False)
```

time: 110 us -> 83.9 us (0.76)
  Pallas kernels: 106 us -> 82.5 us
  local copies, waits for them, and re-layouts: 2.47 us -> 0.67 us
    pallas_call x1, Pallas kernels: 82.9 us -> 69.9 us  [device_step(): pl.pallas_call(step_kernel, out_shape=[jax.ShapeDtypeStruct((shard, batch...]
    pallas_call x1, Pallas kernels: 23.4 us -> 12.6 us  [device_step(): pl.pallas_call(cache_kernel, out_shape=[jax.ShapeDtypeStruct(key_cache.sh...]
    unnamed x9 -> x5, local copies, waits for them, and re-layouts: 2.47 us -> 0.67 us
where the time goes in v2:
time: 83.9 us; the launch traced here: 83.8 us
  Pallas kernels  82.5 us (98%)
    pallas_call x1, Pallas kernels, device_step(): pl.pallas_call(step_kernel, out_shape=[jax.ShapeDtypeStruct((shard, batch...  69.9 us
    pallas_call x1, Pallas kernels, device_step(): pl.pallas_call(cache_kernel, out_shape=[jax.ShapeDtypeStruct(key_cache.sh...  12.6 us

profile of v2, /device:TPU:0, one launch (start us, length us, event | category | flops | bytes accessed | tf_op | source)
XLA Modules:
  0.0 83.8 jit_solution(9597003472305206139)
XLA Ops:
  0.6 0.0 copy-start
  0.6 69.9 %step.1 = (bf16[144,512]{1,0:T(8,128)(2,1)}, f32[2,64,256]{2,1,0:T(8,128)S(1)}, f32[2,64,256]{2,1,0:T(8,128)S(1)}, bf16[2,2,64,256,256]{4,3,2,1,0:T(8,128)(2,1)S(1)}) custom-call(bf16[144,512]{1,0:T(8,128)(2,1)} %bitcast.6, s32[1,64]{1,0:T(1,128)} %bitcast.4, bf16[2,144]{1,0:T(2,128)(2,1)} %ln_in.1, f32[1,128]{1,0:T(1,128)} %constant.3.inv_freq, ...), custom_call_target="tpu_custom_call" | custom-call | tf_op jit(solution)/shard_map/step/pallas_call | solution.py:429
  70.6 0.0 copy-done
  70.6 0.0 copy-start.1
  70.6 12.6 %caches.1 = (bf16[2,64,256,256]{3,2,1,0:T(8,128)(2,1)}, bf16[2,64,256,256]{3,2,1,0:T(8,128)(2,1)}) custom-call(s32[64]{0:T(128)S(1)} %copy-done, f32[2,64,256]{2,1,0:T(8,128)S(1)} %get-tuple-element.10.new_k, f32[2,64,256]{2,1,0:T(8,128)S(1)} %get-tuple-element.11.new_v, bf16[2,2,64,256,256]{4,3,2,1,0:T(8,128)(2,1)S(1)} %get-tuple-element.12.kv_all), custom_call_target="tpu_custom_call" | custom-call | tf_op jit(solution)/shard_map/caches/pallas_call | solution.py:477
  83.2 0.0 copy-done.1
  83.2 0.7 copy.14
Async XLA Ops:
  0.6 69.9 %copy-start = (s32[64]{0:T(128)S(1)}, s32[64]{0:T(128)}, u32[]{:S(2)}) copy-start(s32[64]{0:T(128)} %lengths.1) | copy-start | bytes 772
  70.6 12.6 %copy-start.1 = (bf16[144,512]{1,0:T(8,128)(2,1)S(1)}, bf16[144,512]{1,0:T(8,128)(2,1)}, u32[]{:S(2)}) copy-start(bf16[144,512]{1,0:T(8,128)(2,1)} %get-tuple-element.9) | copy-start | bytes 442372

commit v3 on v2

--- a/solution.py
+++ b/solution.py
@@ -28,11 +28,11 @@
 
 
 def step_kernel(r_in, len_row, ln_in, inv_freq, w_in, w_key, w_val, w_out, k_cache, v_cache,
-                r_out, new_k, new_v, kv_all,
+                sum_d, sum_x, sum_y, base, new_k, new_v, kv_all,
                 w_in_v, w_key_v, w_val_v, w_out_v, w_out_t,
                 r_all, ln_all, ln_col, h_t, joined, y_part, d2d, rs_recv, rs_send,
                 q_send, q_recv, o_send, o_recv, q_rows, s_rows, o_rows, kv_tmp,
-                cos_b, sin_b, len_col, len_rep, perm,
+                cos_b, sin_b, len_col, len_rep, perm, r_buf, r_sem,
                 w_sems, c_sems, ln_ss, ln_rs, ag_ss, ag_rs, q_ss, q_rs, o_ss, o_rs, d_ss, d_rs, t_ss, t_rs):
     layers, width = w_in.shape[0], w_in.shape[2]
     shard, batch = r_in.shape
@@ -63,6 +63,9 @@
     for off in range(1, tp):
         pl.semaphore_signal(barrier, 1, device_id={"tp": (me + off) % tp}, device_id_type=MESH)
 
+    r_load = pltpu.make_async_copy(r_in, r_buf, r_sem)
+    r_load.start()
+
     loads = {}
 
     def load(name, src, dst, sem):
@@ -81,15 +84,11 @@
         load(("k", l), k_cache.at[l], kv_all.at[0, l], c_sems.at[l, 0])
         load(("v", l), v_cache.at[l], kv_all.at[1, l], c_sems.at[l, 1])
 
+    perm[...] = order(cw, cr, rows, batch)
+    r_load.wait()
     load_out(0)
     load_in(0)
-    load_cache(0)
-
-    src_i = iota2((batch, batch), 0)
-    dst_i = iota2((batch, batch), 1)
-    want = ((dst_i % cw) // cr) * rows + (dst_i // cw) * cr + dst_i % cr
-    perm[...] = jnp.where(src_i == want, 1.0, 0.0).astype(BF)
-    r_all[0, me] = dot(r_in[...], perm[...]).astype(BF)
+    r_all[0, me] = dot(r_buf[...], perm[...]).astype(BF)
     ln_all[me] = ln_in[...]
 
     pl.semaphore_wait(barrier, tp - 1)
@@ -145,7 +144,7 @@
             own = iota2((cr, rows), 1) == iota2((cr, rows), 0) + c * cr
             lc = jnp.sum(jnp.where(own, lens, 0.0), axis=1, keepdims=True)
             len_col[c] = lc
-            rep = iota2((hr, rows), 1) == iota2((hr, rows), 0) // heads + c * cr
+            rep = iota2((hr, rows), 1) == lax.shift_right_logical(iota2((hr, rows), 0), heads.bit_length() - 1) + c * cr
             len_rep[c] = jnp.sum(jnp.where(rep, lens, 0.0), axis=1, keepdims=True)
             ang = lc * inv_freq[...]
             cos_b[c] = jnp.cos(ang)
@@ -192,10 +191,10 @@
 
     def feed_forward(l, c):
         cl = pl.ds(c * cw, cw)
-        tile = 288
+        tile = 432
 
         def body(i, _):
-            o = pl.multiple_of(i * tile, 32)
+            o = pl.multiple_of(i * tile, 16)
             gate = dot(w_in_v[pl.ds(o, tile)], h_t[:, cl]).astype(BF).astype(F32)
             up = dot(w_in_v[pl.ds(o + ffn_dev, tile)], h_t[:, cl]).astype(BF).astype(F32)
             joined[pl.ds(o, tile), cl] = (gate * jax.nn.sigmoid(gate) * up).astype(BF)
@@ -215,16 +214,16 @@
             r1.append((x1 * co - x2 * si).astype(BF))
             r2.append((x2 * co + x1 * si).astype(BF))
         ri, ci = iota2((hr, hr), 0), iota2((hr, hr), 1)
-        mix = jnp.where(ci == (ri % heads) * cr + ri // heads, 1.0, 0.0).astype(BF)
+        mix = jnp.where(ci == (ri & (heads - 1)) * cr + lax.shift_right_logical(ri, heads.bit_length() - 1), 1.0, 0.0).astype(BF)
         q_rows[:, :half] = dot(mix, jnp.concatenate(r1, axis=0)).astype(BF)
         q_rows[:, half:] = dot(mix, jnp.concatenate(r2, axis=0)).astype(BF)
-        rep = jnp.where(iota2((hr, cr), 1) == iota2((hr, cr), 0) // heads, 1.0, 0.0).astype(BF)
+        rep = jnp.where(iota2((hr, cr), 1) == lax.shift_right_logical(iota2((hr, cr), 0), heads.bit_length() - 1), 1.0, 0.0).astype(BF)
         k_rep = dot(rep, new_k[l, pl.ds(c * cr, cr)].astype(BF))
         v_rep = dot(rep, new_v[l, pl.ds(c * cr, cr)].astype(BF))
         q_all = q_rows[...].astype(F32)
         s_new = jnp.sum(q_all * k_rep, axis=1, keepdims=True) * head_dim ** -0.5
         group = 16 // heads
-        which = iota2((16, head_dim), 0) // heads
+        which = lax.shift_right_logical(iota2((16, head_dim), 0), heads.bit_length() - 1)
         if c == 0:
             loads[("k", l)].wait()
 
@@ -260,7 +259,7 @@
 
         lax.fori_loop(0, hr // 16, mixv, 0, unroll=4)
         mixed = (o_rows[...] + w_new.astype(BF).astype(F32) * v_rep) / total
-        back = jnp.where(ri == (ci % heads) * cr + ci // heads, 1.0, 0.0).astype(BF)
+        back = jnp.where(ri == (ci & (heads - 1)) * cr + lax.shift_right_logical(ci, heads.bit_length() - 1), 1.0, 0.0).astype(BF)
         heads_o = dot(back, mixed.astype(BF)).astype(BF)
         for t in range(tp):
             o_send[l, c, t] = heads_o[(t // 2) * cr:(t // 2 + 1) * cr, (t % 2) * half:(t % 2 + 1) * half]
@@ -310,6 +309,11 @@
             cp.start()
             sends.append(cp)
 
+    def chip_sums(l, c):
+        for n, (out, dev) in enumerate(((sum_d, dd), (sum_x, dx), (sum_y, dy))):
+            out[:, lanes(c)] = chip_sum(l, c, dev, n).astype(BF)
+        base[:, lanes(c)] = r_all[l, me, :, lanes(c)].astype(F32) + chip_sum(l, c, me, 3)
+
     def rs_last(l, c):
         total = chip_sum(l, c, me, 3)
         for n in (1, 2, 0):
@@ -325,44 +329,64 @@
     ln_start()
     ag_start(0, 0)
     ag_start(0, 1)
+    load_cache(0)
     setup_angles()
     turn_out(0)
     ag_relay(0, 0)
     ln_finish()
     ag_finish(0, 0)
     for l in range(layers):
+        last = l + 1 == layers
         loads[("in", l)].wait()
         norm_query(l, 0)
-        load_cache(l + 1) if l + 1 < layers else None
-        ag_relay(l, 1)
-        ag_finish(l, 1)
-        norm_query(l, 1)
+        if not last:
+            load_cache(l + 1)
         loads[("key", l)].wait()
         loads[("val", l)].wait()
         key_value(l, 0)
+        if l == 0:
+            ag_relay(l, 1)
+            feed_forward(l, 0)
+        else:
+            feed_forward(l, 0)
+            ag_relay(l, 1)
+        ag_finish(l, 1)
+        norm_query(l, 1)
         key_value(l, 1)
-        feed_forward(l, 0)
         attention(l, 0)
-        attention(l, 1)
         feed_forward(l, 1)
-        if l + 1 < layers:
+        if not last:
             load_in(l + 1)
             load_out(l + 1)
+        attention(l, 1)
         project(l, 0)
+        if last:
+            chip_sums(l, 0)
+        else:
+            rs_first(l, 0)
         project(l, 1)
-        rs_first(l, 0)
-        rs_first(l, 1)
-        if l + 1 < layers:
+        if last:
+            chip_sums(l, 1)
+        else:
+            rs_first(l, 1)
             turn_out(l + 1)
             keep(l + 1, 0, rs_last(l, 0))
             keep(l + 1, 1, rs_last(l, 1))
             ag_relay(l + 1, 0)
             ag_finish(l + 1, 0)
-        else:
-            full = jnp.concatenate([rs_last(l, 0), rs_last(l, 1)], axis=1)
-            r_out[...] = dot(full, perm[...], NT).astype(BF)
     for cp in sends:
         cp.wait_send()
+
+
+def order(cw, cr, rows, batch):
+    pos = iota2((1, batch), 1)
+    want = ((pos & (cw - 1)) // cr) * rows + (pos // cw) * cr + (pos & (cr - 1))
+    return jnp.where(iota2((batch, batch), 0) == want, 1.0, 0.0).astype(BF)
+
+
+def final_kernel(cw, cr, rows, base, part_d, part_x, part_y, out):
+    total = base[...] + part_d[...].astype(F32) + part_x[...].astype(F32) + part_y[...].astype(F32)
+    out[...] = dot(total.astype(BF), order(cw, cr, rows, base.shape[1]), NT).astype(BF)
 
 
 def cache_kernel(lengths, new_k, new_v, kv_all, k_out, v_out, tiles, big_sems, tile_sems):
@@ -426,14 +450,15 @@
         hbm = pl.BlockSpec(memory_space=pltpu.HBM)
         smem = pl.BlockSpec(memory_space=pltpu.SMEM)
         dma = pltpu.SemaphoreType.DMA
-        r_new, new_k, new_v, kv_all = pl.pallas_call(
+        sum_d, sum_x, sum_y, base, new_k, new_v, kv_all = pl.pallas_call(
             step_kernel,
-            out_shape=[jax.ShapeDtypeStruct((shard, batch), BF),
+            out_shape=[pltpu.VMEM((shard, batch), BF)] * 3 + [
+                       pltpu.VMEM((shard, batch), F32),
                        pltpu.VMEM((layers, rows, head_dim), F32),
                        pltpu.VMEM((layers, rows, head_dim), F32),
                        pltpu.VMEM((2,) + key_cache.shape, BF)],
-            in_specs=[vmem] * 4 + [hbm] * 6,
-            out_specs=[vmem] * 4,
+            in_specs=[hbm] + [vmem] * 3 + [hbm] * 6,
+            out_specs=[vmem] * 7,
             scratch_shapes=[
                 pltpu.VMEM((in_cols, width), BF),
                 pltpu.VMEM((width, head_dim), BF),
@@ -462,6 +487,8 @@
                 pltpu.VMEM((CHUNKS, cr, 1), F32),
                 pltpu.VMEM((CHUNKS, hr, 1), F32),
                 pltpu.VMEM((batch, batch), BF),
+                pltpu.VMEM((shard, batch), BF),
+                dma,
                 dma((layers, 4)), dma((layers, 2)),
                 dma((tp - 1,)), dma((tp - 1,)),
                 dma((layers, CHUNKS, 7)), dma((layers, CHUNKS, tp)),
@@ -473,6 +500,10 @@
             compiler_params=pltpu.CompilerParams(collective_id=0, has_side_effects=True, vmem_limit_bytes=27 * 2 ** 20),
             name="step",
         )(residual.T, lengths[None, :], ln_scale, inv_freq, jnp.swapaxes(w_in, 1, 2), w_key, w_val, w_out, key_cache, val_cache)
+        def swap(value, bit):
+            return lax.ppermute(value, "tp", [(i, i ^ bit) for i in range(tp)])
+
+        parts = [swap(sum_d, 6), swap(sum_x, 2), swap(sum_y, 4)]
         keep = functools.partial(pltpu.with_memory_space_constraint, memory_space=pltpu.VMEM)
         key_out, val_out = pl.pallas_call(
             cache_kernel,
@@ -483,6 +514,14 @@
             compiler_params=pltpu.CompilerParams(vmem_limit_bytes=5 * 2 ** 20),
             name="caches",
         )(lengths, keep(new_k), keep(new_v), keep(kv_all))
+        r_new = pl.pallas_call(
+            functools.partial(final_kernel, cw, cr, rows),
+            out_shape=jax.ShapeDtypeStruct((shard, batch), BF),
+            in_specs=[vmem] * 4,
+            out_specs=vmem,
+            compiler_params=pltpu.CompilerParams(vmem_limit_bytes=8 * 2 ** 20),
+            name="last",
+        )(keep(base), *parts)
         return r_new.T, key_out, val_out
 
     cache_spec = P(None, ("dp", "tp"), None, None)

time: 83.9 us -> 76.4 us (0.911)
  Pallas kernels: 82.5 us -> 72.1 us
  starting transfers between devices: 0 us -> 3.51 us
    pallas_call x1 -> x2, Pallas kernels: 69.9 us -> 59.5 us  [the longest x1 58.5 us: device_step(): pl.pallas_call(step_kernel, out_shape=[pltpu.VMEM((shard, batch), BF)] *...]
    ppermute x0 -> x3, starting transfers between devices: none -> 3.51 us  [swap(): return lax.ppermute(value, 'tp', [(i, i ^ bit) for i in range(tp)])]
  transfers between devices with their start and end apart: 0 -> 3, of which waited for: 0 -> 0; matrix products, arithmetic and copies ran while one was open for 0% -> 0% of each run, Pallas kernels for 0% -> 16%
where the time goes in v3:
time: 76.4 us; the launch traced here: 76.3 us
  Pallas kernels  72.1 us (94%)
  starting transfers between devices  3.51 us (5%)
    pallas_call x1, Pallas kernels, device_step(): pl.pallas_call(step_kernel, out_shape=[pltpu.VMEM((shard, batch), BF)] *...  58.5 us
    pallas_call x1, Pallas kernels, device_step(): pl.pallas_call(cache_kernel, out_shape=[jax.ShapeDtypeStruct(key_cache.sh...  12.6 us
    ppermute x3, starting transfers between devices, swap(): return lax.ppermute(value, 'tp', [(i, i ^ bit) for i in range(tp)])  3.51 us
  transfers between devices with their start and end apart: 3, of which 0 were waited for; matrix products, arithmetic and copies ran while one was open for 0% of the time, Pallas kernels for 16%

profile of v3, /device:TPU:0, one launch (start us, length us, event | category | flops | bytes accessed | tf_op | source)
XLA Modules:
  0.0 76.3 jit_solution(4611284472583148800)
XLA Ops:
  0.6 0.0 copy-start
  0.6 58.5 %step.1 = (bf16[144,512]{1,0:T(8,128)(2,1)S(1)}, bf16[144,512]{1,0:T(8,128)(2,1)S(1)}, bf16[144,512]{1,0:T(8,128)(2,1)S(1)}, f32[144,512]{1,0:T(8,128)S(1)}, f32...) custom-call(bf16[144,512]{1,0:T(8,128)(2,1)} %bitcast.6, ...), custom_call_target="tpu_custom_call" | custom-call | tf_op jit(solution)/shard_map/step/pallas_call | solution.py:453
  59.1 1.4 %collective-permute-start = (bf16[144,512]{1,0:T(8,128)(2,1)S(1)}, bf16[144,512]{1,0:T(8,128)(2,1)S(1)}, u32[]{:S(2)}, u32[]{:S(2)}) collective-permute-start(bf16[144,512]{1,0:T(8,128)(2,1)S(1)} %get-tuple-element.13), channel_id=1, source_target_pairs={{0,6},{1,7},{2,4},{3,5},{4,2},{5,3},{6,0},{7,1}} | collective-permute-start | bytes 442376 | tf_op jit(solution)/shard_map/ppermute | solution.py:504
  60.6 0.8 %collective-permute-start.1 = (bf16[144,512]{1,0:T(8,128)(2,1)S(1)}, bf16[144,512]{1,0:T(8,128)(2,1)S(1)}, u32[]{:S(2)}, u32[]{:S(2)}) collective-permute-start(bf16[144,512]{1,0:T(8,128)(2,1)S(1)} %get-tuple-element.14), channel_id=1, source_target_pairs={{0,2},{1,3},{2,0},{3,1},{4,6},{5,7},{6,4},{7,5}} | collective-permute-start | bytes 442376 | tf_op jit(solution)/shard_map/ppermute | solution.py:504
  61.3 1.3 %collective-permute-start.2 = (bf16[144,512]{1,0:T(8,128)(2,1)S(1)}, bf16[144,512]{1,0:T(8,128)(2,1)S(1)}, u32[]{:S(2)}, u32[]{:S(2)}) collective-permute-start(bf16[144,512]{1,0:T(8,128)(2,1)S(1)} %get-tuple-element.15), channel_id=1, source_target_pairs={{0,4},{1,5},{2,6},{3,7},{4,0},{5,1},{6,2},{7,3}} | collective-permute-start | bytes 442376 | tf_op jit(solution)/shard_map/ppermute | solution.py:504
  62.6 0.0 copy-done
  62.6 12.6 %caches.1 = (bf16[2,64,256,256]{3,2,1,0:T(8,128)(2,1)}, bf16[2,64,256,256]{3,2,1,0:T(8,128)(2,1)}) custom-call(s32[64]{0:T(128)S(1)} %copy-done, f32[2,64,256]{2,1,0:T(8,128)S(1)} %get-tuple-element.16.new_k, f32[2,64,256]{2,1,0:T(8,128)S(1)} %get-tuple-element.17.new_v, bf16[2,2,64,256,256]{4,3,2,1,0:T(8,128)(2,1)S(1)} %get-tuple-element.18.kv_all), custom_call_target="tpu_custom_call" | custom-call | tf_op jit(solution)/shard_map/caches/pallas_call | solution.py:508
  75.2 0.0 collective-permute-done.part_d
  75.2 0.0 collective-permute-done.1.part_x
  75.2 0.0 collective-permute-done.2.part_y
  75.2 1.0 %last.1 = bf16[144,512]{1,0:T(8,128)(2,1)} custom-call(f32[144,512]{1,0:T(8,128)S(1)} %get-tuple-element.12.base, bf16[144,512]{1,0:T(8,128)(2,1)S(1)} %collective-permute-done.part_d, bf16[144,512]{1,0:T(8,128)(2,1)S(1)} %collective-permute-done.1.part_x, bf16[144,512]{1,0:T(8,128)(2,1)S(1)} %collective-permute-done.2.part_y), custom_call_target="tpu_custom_call" | custom-call | tf_op jit(solution)/shard_map/last/pallas_call | solution.py:517
Async XLA Ops:
  0.6 62.0 %copy-start = (s32[64]{0:T(128)S(1)}, s32[64]{0:T(128)}, u32[]{:S(2)}) copy-start(s32[64]{0:T(128)} %lengths.1) | copy-start | bytes 772
  59.1 16.1 %collective-permute-start = (bf16[144,512]{1,0:T(8,128)(2,1)S(1)}, bf16[144,512]{1,0:T(8,128)(2,1)S(1)}, u32[]{:S(2)}, u32[]{:S(2)}) collective-permute-start(bf16[144,512]{1,0:T(8,128)(2,1)S(1)} %get-tuple-element.13), channel_id=1, source_target_pairs={{0,6},{1,7},{2,4},{3,5},{4,2},{5,3},{6,0},{7,1}} | collective-permute-start | bytes 442376 | tf_op jit(solution)/shard_map/ppermute | solution.py:504
  60.6 14.7 %collective-permute-start.1 = (bf16[144,512]{1,0:T(8,128)(2,1)S(1)}, bf16[144,512]{1,0:T(8,128)(2,1)S(1)}, u32[]{:S(2)}, u32[]{:S(2)}) collective-permute-start(bf16[144,512]{1,0:T(8,128)(2,1)S(1)} %get-tuple-element.14), channel_id=1, source_target_pairs={{0,2},{1,3},{2,0},{3,1},{4,6},{5,7},{6,4},{7,5}} | collective-permute-start | bytes 442376 | tf_op jit(solution)/shard_map/ppermute | solution.py:504
  61.3 13.9 %collective-permute-start.2 = (bf16[144,512]{1,0:T(8,128)(2,1)S(1)}, bf16[144,512]{1,0:T(8,128)(2,1)S(1)}, u32[]{:S(2)}, u32[]{:S(2)}) collective-permute-start(bf16[144,512]{1,0:T(8,128)(2,1)S(1)} %get-tuple-element.15), channel_id=1, source_target_pairs={{0,4},{1,5},{2,6},{3,7},{4,0},{5,1},{6,2},{7,3}} | collective-permute-start | bytes 442376 | tf_op jit(solution)/shard_map/ppermute | solution.py:504

commit v4 on v3

--- a/solution.py
+++ b/solution.py
@@ -93,46 +93,36 @@
 
     pl.semaphore_wait(barrier, tp - 1)
 
-    sends = []
-
     def lanes(c):
         return pl.ds(c * cw, cw)
 
-    def ag_send(l, c, idx, dev, slot):
+    def ag_send(l, c, kind, dev, slot):
         ref = r_all.at[l, slot, :, lanes(c)]
-        cp = rcopy(ref, ref, ag_ss.at[l, c, idx], ag_rs.at[l, c, slot], dev)
-        cp.start()
-        sends.append(cp)
-
-    def ag_wait(l, c, slot):
-        ref = r_all.at[l, slot, :, lanes(c)]
-        rcopy(ref, ref, ag_ss.at[l, c, 0], ag_rs.at[l, c, slot], dp_).wait_recv()
+        rcopy(ref, ref, ag_ss.at[l], ag_rs.at[l, c, kind], dev).start()
+
+    def got(ref, sem):
+        rcopy(ref, ref, ln_ss, sem, dp_).wait_recv()
 
     def ag_start(l, c):
-        ag_send(l, c, 0, dd, me)
-        ag_send(l, c, 1, dx, me)
-        ag_send(l, c, 2, dy, me)
+        ag_send(l, c, 2, dd, me)
+        ag_send(l, c, 0, dx, me)
+        ag_send(l, c, 1, dy, me)
         ag_send(l, c, 3, dp_, me)
 
     def ag_relay(l, c):
         for n, slot in enumerate((dx, dy, dd)):
-            ag_wait(l, c, slot)
-            ag_send(l, c, 4 + n, dp_, slot)
+            got(r_all.at[l, slot, :, lanes(c)], ag_rs.at[l, c, n])
+            ag_send(l, c, 3, dp_, slot)
 
     def ag_finish(l, c):
-        for slot in (dp_, dx + flip, dy + flip, dd + flip):
-            ag_wait(l, c, slot)
+        got(r_all.at[l, pl.ds(0, tp // 2), :, lanes(c)], ag_rs.at[l, c, 3])
 
     def ln_start():
         for off in range(1, tp):
-            cp = rcopy(ln_all.at[me], ln_all.at[me], ln_ss.at[off - 1], ln_rs.at[off - 1], (me + off) % tp)
-            cp.start()
-            sends.append(cp)
+            rcopy(ln_all.at[me], ln_all.at[me], ln_ss, ln_rs, (me + off) % tp).start()
 
     def ln_finish():
-        for off in range(1, tp):
-            ref = ln_all.at[(me + tp - off) % tp]
-            rcopy(ref, ref, ln_ss.at[off - 1], ln_rs.at[off - 1], dp_).wait_recv()
+        got(ln_all.at[pl.ds(0, tp - 1)], ln_rs)
         for l in range(layers):
             pick = jnp.where(iota2((layers, 128), 0) == l, 1.0, 0.0).astype(BF)
             for s in range(tp):
@@ -170,10 +160,7 @@
         q_send[l, cl] = jnp.transpose(q_t).astype(BF)
         for off in range(1, tp):
             dev = (me + off) % tp
-            cp = rcopy(q_send.at[l, pl.ds(c * cw + dev * cr, cr)], q_recv.at[l, c, me],
-                       q_ss.at[l, c, off - 1], q_rs.at[l, c, off - 1], dev)
-            cp.start()
-            sends.append(cp)
+            rcopy(q_send.at[l, pl.ds(c * cw + dev * cr, cr)], q_recv.at[l, c, me], q_ss, q_rs.at[l, c], dev).start()
         q_recv[l, c, me] = q_send[l, pl.ds(pl.multiple_of(c * cw + me * cr, cr), cr)]
 
     def key_value(l, c):
@@ -203,9 +190,7 @@
         lax.fori_loop(0, ffn_dev // tile, body, 0)
 
     def attention(l, c):
-        for off in range(1, tp):
-            ref = q_recv.at[l, c, (me + tp - off) % tp]
-            rcopy(ref, ref, q_ss.at[l, c, off - 1], q_rs.at[l, c, off - 1], dp_).wait_recv()
+        got(q_recv.at[l, c, pl.ds(0, tp - 1)], q_rs.at[l, c])
         co, si = cos_b[c], sin_b[c]
         r1, r2 = [], []
         for h in range(heads):
@@ -265,16 +250,12 @@
             o_send[l, c, t] = heads_o[(t // 2) * cr:(t // 2 + 1) * cr, (t % 2) * half:(t % 2 + 1) * half]
         for off in range(1, tp):
             dev = (me + off) % tp
-            cp = rcopy(o_send.at[l, c, dev], o_recv.at[l, c, me], o_ss.at[l, c, off - 1], o_rs.at[l, c, off - 1], dev)
-            cp.start()
-            sends.append(cp)
+            rcopy(o_send.at[l, c, dev], o_recv.at[l, c, me], o_ss, o_rs.at[l, c], dev).start()
         o_recv[l, c, me] = o_send[l, c, me]
 
     def project(l, c):
         cl = pl.ds(c * cw, cw)
-        for off in range(1, tp):
-            ref = o_recv.at[l, c, (me + tp - off) % tp]
-            rcopy(ref, ref, o_ss.at[l, c, off - 1], o_rs.at[l, c, off - 1], dp_).wait_recv()
+        got(o_recv.at[l, c, pl.ds(0, tp - 1)], o_rs.at[l, c])
         o_all = jnp.concatenate([o_recv[l, c, j].astype(F32) for j in range(tp)], axis=0)
         joined[pl.ds(ffn_dev, q_dev), cl] = jnp.transpose(o_all).astype(BF)
 
@@ -282,9 +263,7 @@
             at = pl.ds(pl.multiple_of(slot * shard, 16), shard)
             y_part[l, at, cl] = dot(w_out_t[at], joined[:, cl]).astype(BF)
             if n < 4:
-                cp = rcopy(y_part.at[l, at, cl], d2d.at[l, slot // 2, :, cl], d_ss.at[l, c, n], d_rs.at[l, c, n], dp_)
-                cp.start()
-                sends.append(cp)
+                rcopy(y_part.at[l, at, cl], d2d.at[l, slot // 2, :, cl], d_ss.at[l], d_rs.at[l, c], dp_).start()
 
     def turn_out(l):
         loads[("out", l)].wait()
@@ -297,17 +276,15 @@
         lax.fori_loop(0, width // 128, body, 0)
 
     def chip_sum(l, c, slot, n):
-        ref = d2d.at[l, slot // 2, :, lanes(c)]
-        rcopy(ref, ref, d_ss.at[l, c, n], d_rs.at[l, c, n], dp_).wait_recv()
+        if n == 0:
+            got(d2d.at[l, :, :, lanes(c)], d_rs.at[l, c])
         mine = y_part[l, pl.ds(pl.multiple_of(slot * shard, 16), shard), lanes(c)].astype(F32)
         return mine + d2d[l, slot // 2, :, lanes(c)].astype(F32)
 
     def rs_first(l, c):
         for n, dev in enumerate((dd, dx, dy)):
             rs_send[l, c, n] = chip_sum(l, c, dev, n).astype(BF)
-            cp = rcopy(rs_send.at[l, c, n], rs_recv.at[l, c, n], t_ss.at[l, c, n], t_rs.at[l, c, n], dev)
-            cp.start()
-            sends.append(cp)
+            rcopy(rs_send.at[l, c, n], rs_recv.at[l, c, n], t_ss, t_rs.at[l, c], dev).start()
 
     def chip_sums(l, c):
         for n, (out, dev) in enumerate(((sum_d, dd), (sum_x, dx), (sum_y, dy))):
@@ -316,9 +293,8 @@
 
     def rs_last(l, c):
         total = chip_sum(l, c, me, 3)
-        for n in (1, 2, 0):
-            ref = rs_recv.at[l, c, n]
-            rcopy(ref, ref, t_ss.at[l, c, n], t_rs.at[l, c, n], dp_).wait_recv()
+        got(rs_recv.at[l, c], t_rs.at[l, c])
+        for n in range(3):
             total = total + rs_recv[l, c, n].astype(F32)
         return (r_all[l, me, :, lanes(c)].astype(F32) + total).astype(BF)
 
@@ -374,8 +350,16 @@
             keep(l + 1, 1, rs_last(l, 1))
             ag_relay(l + 1, 0)
             ag_finish(l + 1, 0)
-    for cp in sends:
-        cp.wait_send()
+    def sent(ref, sem):
+        rcopy(ref, ref, sem, ln_rs, dp_).wait_send()
+
+    sent(ln_all.at[pl.ds(0, tp - 1)], ln_ss)
+    sent(q_send.at[:, pl.ds(0, CHUNKS * (tp - 1) * cr)], q_ss)
+    sent(o_send.at[:, :, pl.ds(0, tp - 1)], o_ss)
+    for l in range(layers):
+        sent(r_all.at[l, pl.ds(0, tp - 1)], ag_ss.at[l])
+        sent(y_part.at[l, pl.ds(0, width // 2)], d_ss.at[l])
+    sent(rs_send, t_ss)
 
 
 def order(cw, cr, rows, batch):
@@ -389,18 +373,36 @@
     out[...] = dot(total.astype(BF), order(cw, cr, rows, base.shape[1]), NT).astype(BF)
 
 
-def cache_kernel(lengths, new_k, new_v, kv_all, k_out, v_out, tiles, big_sems, tile_sems):
+def cache_kernel(lengths, new_k, new_v, kv_all, k_out, v_out, tiles, ends, big_sems, tile_sems):
     layers, rows = kv_all.shape[1:3]
     per = 16
     pairs = [(kv_all.at[0], k_out, new_k, 0), (kv_all.at[1], v_out, new_v, 1)]
     jobs = [(l, g, pair) for l in range(layers) for pair in pairs for g in range(rows // per)]
 
+    n_tail = ends.shape[0]
+    body = len(jobs) - n_tail
+
     def big(i):
         l, g, (src, dst, _, _) = jobs[i]
         at = pl.ds(g * per, per)
-        return pltpu.make_async_copy(src.at[l, at], dst.at[l, at], big_sems.at[i])
-
-    for i in range(len(jobs)):
+        return pltpu.make_async_copy(src.at[l, at] if i < body else ends.at[i - body], dst.at[l, at], big_sems.at[i])
+
+    for i in range(body):
+        big(i).start()
+    for i in range(body, len(jobs)):
+        l, g, (src, _, new, _) = jobs[i]
+
+        def fill(j, _):
+            b = g * per + j
+            slot = lengths[b]
+            base = pl.multiple_of((slot // 16) * 16, 16)
+            hit = iota2((16, kv_all.shape[4]), 0) == slot - base
+            ends[i - body, j] = src[l, b]
+            old = src[l, b, pl.ds(base, 16)].astype(F32)
+            ends[i - body, j, pl.ds(base, 16)] = jnp.where(hit, new[l, pl.ds(b, 1)], old).astype(BF)
+            return 0
+
+        lax.fori_loop(0, per, fill, 0)
         big(i).start()
 
     def build(b, _):
@@ -414,7 +416,7 @@
         return 0
 
     lax.fori_loop(0, rows, build, 0, unroll=4)
-    for i in range(len(jobs)):
+    for i in range(body):
         l, g, (_, dst, _, n) = jobs[i]
         big(i).wait()
 
@@ -426,6 +428,9 @@
 
         lax.fori_loop(0, per, patch, 0, unroll=4)
     for i in range(len(jobs)):
+        if i >= body:
+            big(i).wait()
+            continue
         l, g, (_, dst, _, n) = jobs[i]
         at = pl.ds(g * per, per)
         pltpu.make_async_copy(tiles.at[l, n, at], dst.at[l, at, pl.ds(0, 16)], tile_sems.at[i]).wait()
@@ -472,8 +477,8 @@
                 pltpu.VMEM((ffn_dev + q_dev, batch), BF),
                 pltpu.VMEM((layers, width, batch), BF),
                 pltpu.VMEM((layers, tp // 2, shard, batch), BF),
-                pltpu.VMEM((layers, CHUNKS, 3, shard, cw), BF),
-                pltpu.VMEM((layers, CHUNKS, 3, shard, cw), BF),
+                pltpu.VMEM((layers - 1, CHUNKS, 3, shard, cw), BF),
+                pltpu.VMEM((layers - 1, CHUNKS, 3, shard, cw), BF),
                 pltpu.VMEM((layers, batch, q_dev), BF),
                 pltpu.VMEM((layers, CHUNKS, tp, cr, q_dev), BF),
                 pltpu.VMEM((layers, CHUNKS, tp, cr, q_dev), BF),
@@ -490,12 +495,12 @@
                 pltpu.VMEM((shard, batch), BF),
                 dma,
                 dma((layers, 4)), dma((layers, 2)),
-                dma((tp - 1,)), dma((tp - 1,)),
-                dma((layers, CHUNKS, 7)), dma((layers, CHUNKS, tp)),
-                dma((layers, CHUNKS, tp - 1)), dma((layers, CHUNKS, tp - 1)),
-                dma((layers, CHUNKS, tp - 1)), dma((layers, CHUNKS, tp - 1)),
-                dma((layers, CHUNKS, 4)), dma((layers, CHUNKS, 4)),
-                dma((layers, CHUNKS, 3)), dma((layers, CHUNKS, 3)),
+                dma, dma,
+                dma((layers,)), dma((layers, CHUNKS, 4)),
+                dma, dma((layers, CHUNKS)),
+                dma, dma((layers, CHUNKS)),
+                dma((layers,)), dma((layers, CHUNKS)),
+                dma, dma((layers - 1, CHUNKS)),
             ],
             compiler_params=pltpu.CompilerParams(collective_id=0, has_side_effects=True, vmem_limit_bytes=27 * 2 ** 20),
             name="step",
@@ -510,8 +515,8 @@
             out_shape=[jax.ShapeDtypeStruct(key_cache.shape, BF)] * 2,
             in_specs=[smem] + [vmem] * 3,
             out_specs=[hbm, hbm],
-            scratch_shapes=[pltpu.VMEM((layers, 2, rows, 16, head_dim), BF), dma((16,)), dma((16,))],
-            compiler_params=pltpu.CompilerParams(vmem_limit_bytes=5 * 2 ** 20),
+            scratch_shapes=[pltpu.VMEM((layers, 2, rows, 16, head_dim), BF), pltpu.VMEM((2, 16, slots, head_dim), BF), dma((16,)), dma((14,))],
+            compiler_params=pltpu.CompilerParams(vmem_limit_bytes=9 * 2 ** 20),
             name="caches",
         )(lengths, keep(new_k), keep(new_v), keep(kv_all))
         r_new = pl.pallas_call(

time: 76.4 us -> 75 us (0.982)
  Pallas kernels: 72.1 us -> 70.7 us
    pallas_call x1, Pallas kernels: 58.5 us -> 57.2 us  [device_step(): pl.pallas_call(step_kernel, out_shape=[pltpu.VMEM((shard, batch), BF)] *...]
  transfers between devices with their start and end apart: 3 -> 3, of which waited for: 0 -> 0; matrix products, arithmetic and copies ran while one was open for 0% -> 0% of each run, Pallas kernels for 16% -> 17%
where the time goes in v4:
time: 75 us; the launch traced here: 74.9 us
  Pallas kernels  70.7 us (94%)
  starting transfers between devices  3.51 us (5%)
    pallas_call x1, Pallas kernels, device_step(): pl.pallas_call(step_kernel, out_shape=[pltpu.VMEM((shard, batch), BF)] *...  57.2 us
    pallas_call x1, Pallas kernels, device_step(): pl.pallas_call(cache_kernel, out_shape=[jax.ShapeDtypeStruct(key_cache.sh...  12.4 us
    ppermute x3, starting transfers between devices, swap(): return lax.ppermute(value, 'tp', [(i, i ^ bit) for i in range(tp)])  3.51 us
  transfers between devices with their start and end apart: 3, of which 0 were waited for; matrix products, arithmetic and copies ran while one was open for 0% of the time, Pallas kernels for 17%

profile of v4, /device:TPU:0, one launch (start us, length us, event | category | flops | bytes accessed | tf_op | source)
XLA Modules:
  0.0 74.9 jit_solution(16683401978838569761)
XLA Ops:
  0.6 0.0 copy-start
  0.6 57.2 %step.1 = (bf16[144,512]{1,0:T(8,128)(2,1)S(1)}, bf16[144,512]{1,0:T(8,128)(2,1)S(1)}, bf16[144,512]{1,0:T(8,128)(2,1)S(1)}, f32[144,512]{1,0:T(8,128)S(1)}, f32...) custom-call(bf16[144,512]{1,0:T(8,128)(2,1)} %bitcast.6, ...), custom_call_target="tpu_custom_call" | custom-call | tf_op jit(solution)/shard_map/step/pallas_call | solution.py:458
  57.9 1.3 %collective-permute-start = (bf16[144,512]{1,0:T(8,128)(2,1)S(1)}, bf16[144,512]{1,0:T(8,128)(2,1)S(1)}, u32[]{:S(2)}, u32[]{:S(2)}) collective-permute-start(bf16[144,512]{1,0:T(8,128)(2,1)S(1)} %get-tuple-element.13), channel_id=1, source_target_pairs={{0,6},{1,7},{2,4},{3,5},{4,2},{5,3},{6,0},{7,1}} | collective-permute-start | bytes 442376 | tf_op jit(solution)/shard_map/ppermute | solution.py:509
  59.2 0.9 %collective-permute-start.1 = (bf16[144,512]{1,0:T(8,128)(2,1)S(1)}, bf16[144,512]{1,0:T(8,128)(2,1)S(1)}, u32[]{:S(2)}, u32[]{:S(2)}) collective-permute-start(bf16[144,512]{1,0:T(8,128)(2,1)S(1)} %get-tuple-element.14), channel_id=1, source_target_pairs={{0,2},{1,3},{2,0},{3,1},{4,6},{5,7},{6,4},{7,5}} | collective-permute-start | bytes 442376 | tf_op jit(solution)/shard_map/ppermute | solution.py:509
  60.1 1.3 %collective-permute-start.2 = (bf16[144,512]{1,0:T(8,128)(2,1)S(1)}, bf16[144,512]{1,0:T(8,128)(2,1)S(1)}, u32[]{:S(2)}, u32[]{:S(2)}) collective-permute-start(bf16[144,512]{1,0:T(8,128)(2,1)S(1)} %get-tuple-element.15), channel_id=1, source_target_pairs={{0,4},{1,5},{2,6},{3,7},{4,0},{5,1},{6,2},{7,3}} | collective-permute-start | bytes 442376 | tf_op jit(solution)/shard_map/ppermute | solution.py:509
  61.4 0.0 copy-done
  61.4 12.4 %caches.1 = (bf16[2,64,256,256]{3,2,1,0:T(8,128)(2,1)}, bf16[2,64,256,256]{3,2,1,0:T(8,128)(2,1)}) custom-call(s32[64]{0:T(128)S(1)} %copy-done, f32[2,64,256]{2,1,0:T(8,128)S(1)} %get-tuple-element.16.new_k, f32[2,64,256]{2,1,0:T(8,128)S(1)} %get-tuple-element.17.new_v, bf16[2,2,64,256,256]{4,3,2,1,0:T(8,128)(2,1)S(1)} %get-tuple-element.18.kv_all), custom_call_target="tpu_custom_call" | custom-call | tf_op jit(solution)/shard_map/caches/pallas_call | solution.py:513
  73.8 0.0 collective-permute-done.part_d
  73.9 0.0 collective-permute-done.1.part_x
  73.9 0.0 collective-permute-done.2.part_y
  73.9 1.0 %last.1 = bf16[144,512]{1,0:T(8,128)(2,1)} custom-call(f32[144,512]{1,0:T(8,128)S(1)} %get-tuple-element.12.base, bf16[144,512]{1,0:T(8,128)(2,1)S(1)} %collective-permute-done.part_d, bf16[144,512]{1,0:T(8,128)(2,1)S(1)} %collective-permute-done.1.part_x, bf16[144,512]{1,0:T(8,128)(2,1)S(1)} %collective-permute-done.2.part_y), custom_call_target="tpu_custom_call" | custom-call | tf_op jit(solution)/shard_map/last/pallas_call | solution.py:522
Async XLA Ops:
  0.6 60.8 %copy-start = (s32[64]{0:T(128)S(1)}, s32[64]{0:T(128)}, u32[]{:S(2)}) copy-start(s32[64]{0:T(128)} %lengths.1) | copy-start | bytes 772
  57.9 16.0 %collective-permute-start = (bf16[144,512]{1,0:T(8,128)(2,1)S(1)}, bf16[144,512]{1,0:T(8,128)(2,1)S(1)}, u32[]{:S(2)}, u32[]{:S(2)}) collective-permute-start(bf16[144,512]{1,0:T(8,128)(2,1)S(1)} %get-tuple-element.13), channel_id=1, source_target_pairs={{0,6},{1,7},{2,4},{3,5},{4,2},{5,3},{6,0},{7,1}} | collective-permute-start | bytes 442376 | tf_op jit(solution)/shard_map/ppermute | solution.py:509
  59.2 14.7 %collective-permute-start.1 = (bf16[144,512]{1,0:T(8,128)(2,1)S(1)}, bf16[144,512]{1,0:T(8,128)(2,1)S(1)}, u32[]{:S(2)}, u32[]{:S(2)}) collective-permute-start(bf16[144,512]{1,0:T(8,128)(2,1)S(1)} %get-tuple-element.14), channel_id=1, source_target_pairs={{0,2},{1,3},{2,0},{3,1},{4,6},{5,7},{6,4},{7,5}} | collective-permute-start | bytes 442376 | tf_op jit(solution)/shard_map/ppermute | solution.py:509
  60.1 13.8 %collective-permute-start.2 = (bf16[144,512]{1,0:T(8,128)(2,1)S(1)}, bf16[144,512]{1,0:T(8,128)(2,1)S(1)}, u32[]{:S(2)}, u32[]{:S(2)}) collective-permute-start(bf16[144,512]{1,0:T(8,128)(2,1)S(1)} %get-tuple-element.15), channel_id=1, source_target_pairs={{0,4},{1,5},{2,6},{3,7},{4,0},{5,1},{6,2},{7,3}} | collective-permute-start | bytes 442376 | tf_op jit(solution)/shard_map/ppermute | solution.py:509

commit v5 on v4

--- a/solution.py
+++ b/solution.py
@@ -178,16 +178,9 @@
 
     def feed_forward(l, c):
         cl = pl.ds(c * cw, cw)
-        tile = 432
-
-        def body(i, _):
-            o = pl.multiple_of(i * tile, 16)
-            gate = dot(w_in_v[pl.ds(o, tile)], h_t[:, cl]).astype(BF).astype(F32)
-            up = dot(w_in_v[pl.ds(o + ffn_dev, tile)], h_t[:, cl]).astype(BF).astype(F32)
-            joined[pl.ds(o, tile), cl] = (gate * jax.nn.sigmoid(gate) * up).astype(BF)
-            return 0
-
-        lax.fori_loop(0, ffn_dev // tile, body, 0)
+        gate = dot(w_in_v[pl.ds(0, ffn_dev)], h_t[:, cl]).astype(BF).astype(F32)
+        up = dot(w_in_v[pl.ds(ffn_dev, ffn_dev)], h_t[:, cl]).astype(BF).astype(F32)
+        joined[pl.ds(0, ffn_dev), cl] = (gate * jax.nn.sigmoid(gate) * up).astype(BF)
 
     def attention(l, c):
         got(q_recv.at[l, c, pl.ds(0, tp - 1)], q_rs.at[l, c])
@@ -221,7 +214,7 @@
             s_rows[pl.ds(o, 16)] = acc
             return 0
 
-        lax.fori_loop(0, hr // 16, score, 0, unroll=4)
+        lax.fori_loop(0, hr // 16, score, 0, unroll=hr // 16)
         s = s_rows[...] * head_dim ** -0.5
         pos = iota2((hr, s.shape[1]), 1).astype(F32)
         s = jnp.where(pos < len_rep[c], s, -1e30)
@@ -242,7 +235,7 @@
             o_rows[pl.ds(o, 16)] = acc
             return 0
 
-        lax.fori_loop(0, hr // 16, mixv, 0, unroll=4)
+        lax.fori_loop(0, hr // 16, mixv, 0, unroll=hr // 16)
         mixed = (o_rows[...] + w_new.astype(BF).astype(F32) * v_rep) / total
         back = jnp.where(ri == (ci & (heads - 1)) * cr + lax.shift_right_logical(ci, heads.bit_length() - 1), 1.0, 0.0).astype(BF)
         heads_o = dot(back, mixed.astype(BF)).astype(BF)
@@ -330,26 +323,28 @@
         norm_query(l, 1)
         key_value(l, 1)
         attention(l, 0)
-        feed_forward(l, 1)
         if not last:
+            feed_forward(l, 1)
             load_in(l + 1)
             load_out(l + 1)
         attention(l, 1)
+        if last:
+            feed_forward(l, 1)
         project(l, 0)
         if last:
+            project(l, 1)
             chip_sums(l, 0)
+            chip_sums(l, 1)
         else:
             rs_first(l, 0)
-        project(l, 1)
-        if last:
-            chip_sums(l, 1)
-        else:
+            project(l, 1)
             rs_first(l, 1)
+            keep(l + 1, 0, rs_last(l, 0))
             turn_out(l + 1)
-            keep(l + 1, 0, rs_last(l, 0))
             keep(l + 1, 1, rs_last(l, 1))
             ag_relay(l + 1, 0)
             ag_finish(l + 1, 0)
+
     def sent(ref, sem):
         rcopy(ref, ref, sem, ln_rs, dp_).wait_send()
 

time: 75 us -> 70.1 us (0.935)
  Pallas kernels: 70.7 us -> 65.8 us
    pallas_call x1, Pallas kernels: 57.2 us -> 52.3 us  [device_step(): pl.pallas_call(step_kernel, out_shape=[pltpu.VMEM((shard, batch), BF)] *...]
  transfers between devices with their start and end apart: 3 -> 3, of which waited for: 0 -> 0; matrix products, arithmetic and copies ran while one was open for 0% -> 0% of each run, Pallas kernels for 17% -> 18%
where the time goes in v5:
time: 70.1 us; the launch traced here: 70 us
  Pallas kernels  65.8 us (94%)
  starting transfers between devices  3.51 us (5%)
    pallas_call x1, Pallas kernels, device_step(): pl.pallas_call(step_kernel, out_shape=[pltpu.VMEM((shard, batch), BF)] *...  52.3 us
    pallas_call x1, Pallas kernels, device_step(): pl.pallas_call(cache_kernel, out_shape=[jax.ShapeDtypeStruct(key_cache.sh...  12.4 us
    ppermute x3, starting transfers between devices, swap(): return lax.ppermute(value, 'tp', [(i, i ^ bit) for i in range(tp)])  3.51 us
  transfers between devices with their start and end apart: 3, of which 0 were waited for; matrix products, arithmetic and copies ran while one was open for 0% of the time, Pallas kernels for 18%

profile of v5, /device:TPU:0, one launch (start us, length us, event | category | flops | bytes accessed | tf_op | source)
XLA Modules:
  0.0 70.0 jit_solution(6472080095167724979)
XLA Ops:
  0.6 0.0 copy-start
  0.6 52.3 %step.1 = (bf16[144,512]{1,0:T(8,128)(2,1)S(1)}, bf16[144,512]{1,0:T(8,128)(2,1)S(1)}, bf16[144,512]{1,0:T(8,128)(2,1)S(1)}, f32[144,512]{1,0:T(8,128)S(1)}, f32...) custom-call(bf16[144,512]{1,0:T(8,128)(2,1)} %bitcast.6, ...), custom_call_target="tpu_custom_call" | custom-call | tf_op jit(solution)/shard_map/step/pallas_call | solution.py:453
  53.0 1.5 %collective-permute-start = (bf16[144,512]{1,0:T(8,128)(2,1)S(1)}, bf16[144,512]{1,0:T(8,128)(2,1)S(1)}, u32[]{:S(2)}, u32[]{:S(2)}) collective-permute-start(bf16[144,512]{1,0:T(8,128)(2,1)S(1)} %get-tuple-element.13), channel_id=1, source_target_pairs={{0,6},{1,7},{2,4},{3,5},{4,2},{5,3},{6,0},{7,1}} | collective-permute-start | bytes 442376 | tf_op jit(solution)/shard_map/ppermute | solution.py:504
  54.5 0.7 %collective-permute-start.1 = (bf16[144,512]{1,0:T(8,128)(2,1)S(1)}, bf16[144,512]{1,0:T(8,128)(2,1)S(1)}, u32[]{:S(2)}, u32[]{:S(2)}) collective-permute-start(bf16[144,512]{1,0:T(8,128)(2,1)S(1)} %get-tuple-element.14), channel_id=1, source_target_pairs={{0,2},{1,3},{2,0},{3,1},{4,6},{5,7},{6,4},{7,5}} | collective-permute-start | bytes 442376 | tf_op jit(solution)/shard_map/ppermute | solution.py:504
  55.2 1.3 %collective-permute-start.2 = (bf16[144,512]{1,0:T(8,128)(2,1)S(1)}, bf16[144,512]{1,0:T(8,128)(2,1)S(1)}, u32[]{:S(2)}, u32[]{:S(2)}) collective-permute-start(bf16[144,512]{1,0:T(8,128)(2,1)S(1)} %get-tuple-element.15), channel_id=1, source_target_pairs={{0,4},{1,5},{2,6},{3,7},{4,0},{5,1},{6,2},{7,3}} | collective-permute-start | bytes 442376 | tf_op jit(solution)/shard_map/ppermute | solution.py:504
  56.5 0.0 copy-done
  56.5 12.4 %caches.1 = (bf16[2,64,256,256]{3,2,1,0:T(8,128)(2,1)}, bf16[2,64,256,256]{3,2,1,0:T(8,128)(2,1)}) custom-call(s32[64]{0:T(128)S(1)} %copy-done, f32[2,64,256]{2,1,0:T(8,128)S(1)} %get-tuple-element.16.new_k, f32[2,64,256]{2,1,0:T(8,128)S(1)} %get-tuple-element.17.new_v, bf16[2,2,64,256,256]{4,3,2,1,0:T(8,128)(2,1)S(1)} %get-tuple-element.18.kv_all), custom_call_target="tpu_custom_call" | custom-call | tf_op jit(solution)/shard_map/caches/pallas_call | solution.py:508
  68.9 0.0 collective-permute-done.part_d
  68.9 0.0 collective-permute-done.1.part_x
  68.9 0.0 collective-permute-done.2.part_y
  68.9 1.0 %last.1 = bf16[144,512]{1,0:T(8,128)(2,1)} custom-call(f32[144,512]{1,0:T(8,128)S(1)} %get-tuple-element.12.base, bf16[144,512]{1,0:T(8,128)(2,1)S(1)} %collective-permute-done.part_d, bf16[144,512]{1,0:T(8,128)(2,1)S(1)} %collective-permute-done.1.part_x, bf16[144,512]{1,0:T(8,128)(2,1)S(1)} %collective-permute-done.2.part_y), custom_call_target="tpu_custom_call" | custom-call | tf_op jit(solution)/shard_map/last/pallas_call | solution.py:517
Async XLA Ops:
  0.6 55.8 %copy-start = (s32[64]{0:T(128)S(1)}, s32[64]{0:T(128)}, u32[]{:S(2)}) copy-start(s32[64]{0:T(128)} %lengths.1) | copy-start | bytes 772
  53.0 16.0 %collective-permute-start = (bf16[144,512]{1,0:T(8,128)(2,1)S(1)}, bf16[144,512]{1,0:T(8,128)(2,1)S(1)}, u32[]{:S(2)}, u32[]{:S(2)}) collective-permute-start(bf16[144,512]{1,0:T(8,128)(2,1)S(1)} %get-tuple-element.13), channel_id=1, source_target_pairs={{0,6},{1,7},{2,4},{3,5},{4,2},{5,3},{6,0},{7,1}} | collective-permute-start | bytes 442376 | tf_op jit(solution)/shard_map/ppermute | solution.py:504
  54.5 14.5 %collective-permute-start.1 = (bf16[144,512]{1,0:T(8,128)(2,1)S(1)}, bf16[144,512]{1,0:T(8,128)(2,1)S(1)}, u32[]{:S(2)}, u32[]{:S(2)}) collective-permute-start(bf16[144,512]{1,0:T(8,128)(2,1)S(1)} %get-tuple-element.14), channel_id=1, source_target_pairs={{0,2},{1,3},{2,0},{3,1},{4,6},{5,7},{6,4},{7,5}} | collective-permute-start | bytes 442376 | tf_op jit(solution)/shard_map/ppermute | solution.py:504
  55.2 13.7 %collective-permute-start.2 = (bf16[144,512]{1,0:T(8,128)(2,1)S(1)}, bf16[144,512]{1,0:T(8,128)(2,1)S(1)}, u32[]{:S(2)}, u32[]{:S(2)}) collective-permute-start(bf16[144,512]{1,0:T(8,128)(2,1)S(1)} %get-tuple-element.15), channel_id=1, source_target_pairs={{0,4},{1,5},{2,6},{3,7},{4,0},{5,1},{6,2},{7,3}} | collective-permute-start | bytes 442376 | tf_op jit(solution)/shard_map/ppermute | solution.py:504

commit v6 on v5

--- a/solution.py
+++ b/solution.py
@@ -54,6 +54,7 @@
     dy = me + 4 - 8 * ypos
     dd = dx + 4 - 8 * ypos
     flip = 1 - 2 * core
+    others = (dd + flip, dd, dx + flip, dy + flip, dx, dy, dp_)
 
     def rcopy(src, dst, ss, rs, dev):
         return pltpu.make_async_remote_copy(src_ref=src, dst_ref=dst, send_sem=ss, recv_sem=rs,
@@ -158,8 +159,7 @@
             h_t[pl.ds(s * shard, shard), cl] = ((v - mean) * inv * scale).astype(BF)
         q_t = dot(w_in_v[pl.ds(2 * ffn_dev, q_dev), :], h_t[:, cl])
         q_send[l, cl] = jnp.transpose(q_t).astype(BF)
-        for off in range(1, tp):
-            dev = (me + off) % tp
+        for dev in others:
             rcopy(q_send.at[l, pl.ds(c * cw + dev * cr, cr)], q_recv.at[l, c, me], q_ss, q_rs.at[l, c], dev).start()
         q_recv[l, c, me] = q_send[l, pl.ds(pl.multiple_of(c * cw + me * cr, cr), cr)]
 
@@ -241,8 +241,7 @@
         heads_o = dot(back, mixed.astype(BF)).astype(BF)
         for t in range(tp):
             o_send[l, c, t] = heads_o[(t // 2) * cr:(t // 2 + 1) * cr, (t % 2) * half:(t % 2 + 1) * half]
-        for off in range(1, tp):
-            dev = (me + off) % tp
+        for dev in others:
             rcopy(o_send.at[l, c, dev], o_recv.at[l, c, me], o_ss, o_rs.at[l, c], dev).start()
         o_recv[l, c, me] = o_send[l, c, me]
 
@@ -301,8 +300,8 @@
     load_cache(0)
     setup_angles()
     turn_out(0)
+    ln_finish()
     ag_relay(0, 0)
-    ln_finish()
     ag_finish(0, 0)
     for l in range(layers):
         last = l + 1 == layers

time: 70.1 us -> 69.5 us (level)
  no operation moved by 1% of the time
where the time goes in v6:
time: 69.5 us; the launch traced here: 69.4 us
  Pallas kernels  65.2 us (94%)
  starting transfers between devices  3.51 us (5%)
    pallas_call x1, Pallas kernels, device_step(): pl.pallas_call(step_kernel, out_shape=[pltpu.VMEM((shard, batch), BF)] *...  51.7 us
    pallas_call x1, Pallas kernels, device_step(): pl.pallas_call(cache_kernel, out_shape=[jax.ShapeDtypeStruct(key_cache.sh...  12.4 us
    ppermute x3, starting transfers between devices, swap(): return lax.ppermute(value, 'tp', [(i, i ^ bit) for i in range(tp)])  3.51 us
  transfers between devices with their start and end apart: 3, of which 0 were waited for; matrix products, arithmetic and copies ran while one was open for 0% of the time, Pallas kernels for 18%

profile of v6, /device:TPU:0, one launch (start us, length us, event | category | flops | bytes accessed | tf_op | source)
XLA Modules:
  0.0 69.4 jit_solution(15152225280762976487)
XLA Ops:
  0.6 0.0 copy-start
  0.6 51.7 %step.1 = (bf16[144,512]{1,0:T(8,128)(2,1)S(1)}, bf16[144,512]{1,0:T(8,128)(2,1)S(1)}, bf16[144,512]{1,0:T(8,128)(2,1)S(1)}, f32[144,512]{1,0:T(8,128)S(1)}, f32...) custom-call(bf16[144,512]{1,0:T(8,128)(2,1)} %bitcast.6, ...), custom_call_target="tpu_custom_call" | custom-call | tf_op jit(solution)/shard_map/step/pallas_call | solution.py:452
  52.4 1.3 %collective-permute-start = (bf16[144,512]{1,0:T(8,128)(2,1)S(1)}, bf16[144,512]{1,0:T(8,128)(2,1)S(1)}, u32[]{:S(2)}, u32[]{:S(2)}) collective-permute-start(bf16[144,512]{1,0:T(8,128)(2,1)S(1)} %get-tuple-element.13), channel_id=1, source_target_pairs={{0,6},{1,7},{2,4},{3,5},{4,2},{5,3},{6,0},{7,1}} | collective-permute-start | bytes 442376 | tf_op jit(solution)/shard_map/ppermute | solution.py:503
  53.7 1.2 %collective-permute-start.1 = (bf16[144,512]{1,0:T(8,128)(2,1)S(1)}, bf16[144,512]{1,0:T(8,128)(2,1)S(1)}, u32[]{:S(2)}, u32[]{:S(2)}) collective-permute-start(bf16[144,512]{1,0:T(8,128)(2,1)S(1)} %get-tuple-element.14), channel_id=1, source_target_pairs={{0,2},{1,3},{2,0},{3,1},{4,6},{5,7},{6,4},{7,5}} | collective-permute-start | bytes 442376 | tf_op jit(solution)/shard_map/ppermute | solution.py:503
  54.9 1.0 %collective-permute-start.2 = (bf16[144,512]{1,0:T(8,128)(2,1)S(1)}, bf16[144,512]{1,0:T(8,128)(2,1)S(1)}, u32[]{:S(2)}, u32[]{:S(2)}) collective-permute-start(bf16[144,512]{1,0:T(8,128)(2,1)S(1)} %get-tuple-element.15), channel_id=1, source_target_pairs={{0,4},{1,5},{2,6},{3,7},{4,0},{5,1},{6,2},{7,3}} | collective-permute-start | bytes 442376 | tf_op jit(solution)/shard_map/ppermute | solution.py:503
  55.9 0.0 copy-done
  55.9 12.4 %caches.1 = (bf16[2,64,256,256]{3,2,1,0:T(8,128)(2,1)}, bf16[2,64,256,256]{3,2,1,0:T(8,128)(2,1)}) custom-call(s32[64]{0:T(128)S(1)} %copy-done, f32[2,64,256]{2,1,0:T(8,128)S(1)} %get-tuple-element.16.new_k, f32[2,64,256]{2,1,0:T(8,128)S(1)} %get-tuple-element.17.new_v, bf16[2,2,64,256,256]{4,3,2,1,0:T(8,128)(2,1)S(1)} %get-tuple-element.18.kv_all), custom_call_target="tpu_custom_call" | custom-call | tf_op jit(solution)/shard_map/caches/pallas_call | solution.py:507
  68.3 0.0 collective-permute-done.part_d
  68.3 0.0 collective-permute-done.1.part_x
  68.4 0.0 collective-permute-done.2.part_y
  68.4 1.0 %last.1 = bf16[144,512]{1,0:T(8,128)(2,1)} custom-call(f32[144,512]{1,0:T(8,128)S(1)} %get-tuple-element.12.base, bf16[144,512]{1,0:T(8,128)(2,1)S(1)} %collective-permute-done.part_d, bf16[144,512]{1,0:T(8,128)(2,1)S(1)} %collective-permute-done.1.part_x, bf16[144,512]{1,0:T(8,128)(2,1)S(1)} %collective-permute-done.2.part_y), custom_call_target="tpu_custom_call" | custom-call | tf_op jit(solution)/shard_map/last/pallas_call | solution.py:516
Async XLA Ops:
  0.6 55.3 %copy-start = (s32[64]{0:T(128)S(1)}, s32[64]{0:T(128)}, u32[]{:S(2)}) copy-start(s32[64]{0:T(128)} %lengths.1) | copy-start | bytes 772
  52.4 16.0 %collective-permute-start = (bf16[144,512]{1,0:T(8,128)(2,1)S(1)}, bf16[144,512]{1,0:T(8,128)(2,1)S(1)}, u32[]{:S(2)}, u32[]{:S(2)}) collective-permute-start(bf16[144,512]{1,0:T(8,128)(2,1)S(1)} %get-tuple-element.13), channel_id=1, source_target_pairs={{0,6},{1,7},{2,4},{3,5},{4,2},{5,3},{6,0},{7,1}} | collective-permute-start | bytes 442376 | tf_op jit(solution)/shard_map/ppermute | solution.py:503
  53.7 14.6 %collective-permute-start.1 = (bf16[144,512]{1,0:T(8,128)(2,1)S(1)}, bf16[144,512]{1,0:T(8,128)(2,1)S(1)}, u32[]{:S(2)}, u32[]{:S(2)}) collective-permute-start(bf16[144,512]{1,0:T(8,128)(2,1)S(1)} %get-tuple-element.14), channel_id=1, source_target_pairs={{0,2},{1,3},{2,0},{3,1},{4,6},{5,7},{6,4},{7,5}} | collective-permute-start | bytes 442376 | tf_op jit(solution)/shard_map/ppermute | solution.py:503
  54.9 13.5 %collective-permute-start.2 = (bf16[144,512]{1,0:T(8,128)(2,1)S(1)}, bf16[144,512]{1,0:T(8,128)(2,1)S(1)}, u32[]{:S(2)}, u32[]{:S(2)}) collective-permute-start(bf16[144,512]{1,0:T(8,128)(2,1)S(1)} %get-tuple-element.15), channel_id=1, source_target_pairs={{0,4},{1,5},{2,6},{3,7},{4,0},{5,1},{6,2},{7,3}} | collective-permute-start | bytes 442376 | tf_op jit(solution)/shard_map/ppermute | solution.py:503

commit v7 on v6

--- a/solution.py
+++ b/solution.py
@@ -509,8 +509,8 @@
             out_shape=[jax.ShapeDtypeStruct(key_cache.shape, BF)] * 2,
             in_specs=[smem] + [vmem] * 3,
             out_specs=[hbm, hbm],
-            scratch_shapes=[pltpu.VMEM((layers, 2, rows, 16, head_dim), BF), pltpu.VMEM((2, 16, slots, head_dim), BF), dma((16,)), dma((14,))],
-            compiler_params=pltpu.CompilerParams(vmem_limit_bytes=9 * 2 ** 20),
+            scratch_shapes=[pltpu.VMEM((layers, 2, rows, 16, head_dim), BF), pltpu.VMEM((8, 16, slots, head_dim), BF), dma((16,)), dma((8,))],
+            compiler_params=pltpu.CompilerParams(vmem_limit_bytes=21 * 2 ** 20),
             name="caches",
         )(lengths, keep(new_k), keep(new_v), keep(kv_all))
         r_new = pl.pallas_call(

time: 69.5 us -> 69.1 us (level)
  transfers between devices with their start and end apart: 3 -> 3, of which waited for: 0 -> 0; matrix products, arithmetic and copies ran while one was open for 0% -> 0% of each run, Pallas kernels for 18% -> 17%
where the time goes in v7:
time: 69.1 us; the launch traced here: 69 us
  Pallas kernels  64.8 us (94%)
  starting transfers between devices  3.51 us (5%)
    pallas_call x1, Pallas kernels, device_step(): pl.pallas_call(step_kernel, out_shape=[pltpu.VMEM((shard, batch), BF)] *...  51.7 us
    pallas_call x1, Pallas kernels, device_step(): pl.pallas_call(cache_kernel, out_shape=[jax.ShapeDtypeStruct(key_cache.sh...  12 us
    ppermute x3, starting transfers between devices, swap(): return lax.ppermute(value, 'tp', [(i, i ^ bit) for i in range(tp)])  3.51 us
  transfers between devices with their start and end apart: 3, of which 0 were waited for; matrix products, arithmetic and copies ran while one was open for 0% of the time, Pallas kernels for 17%

profile of v7, /device:TPU:0, one launch (start us, length us, event | category | flops | bytes accessed | tf_op | source)
XLA Modules:
  0.0 69.0 jit_solution(8937543707212427300)
XLA Ops:
  0.6 0.0 copy-start
  0.6 51.7 %step.1 = (bf16[144,512]{1,0:T(8,128)(2,1)S(1)}, bf16[144,512]{1,0:T(8,128)(2,1)S(1)}, bf16[144,512]{1,0:T(8,128)(2,1)S(1)}, f32[144,512]{1,0:T(8,128)S(1)}, f32...) custom-call(bf16[144,512]{1,0:T(8,128)(2,1)} %bitcast.6, ...), custom_call_target="tpu_custom_call" | custom-call | tf_op jit(solution)/shard_map/step/pallas_call | solution.py:452
  52.4 1.3 %collective-permute-start = (bf16[144,512]{1,0:T(8,128)(2,1)S(1)}, bf16[144,512]{1,0:T(8,128)(2,1)S(1)}, u32[]{:S(2)}, u32[]{:S(2)}) collective-permute-start(bf16[144,512]{1,0:T(8,128)(2,1)S(1)} %get-tuple-element.13), channel_id=1, source_target_pairs={{0,6},{1,7},{2,4},{3,5},{4,2},{5,3},{6,0},{7,1}} | collective-permute-start | bytes 442376 | tf_op jit(solution)/shard_map/ppermute | solution.py:503
  53.7 1.2 %collective-permute-start.1 = (bf16[144,512]{1,0:T(8,128)(2,1)S(1)}, bf16[144,512]{1,0:T(8,128)(2,1)S(1)}, u32[]{:S(2)}, u32[]{:S(2)}) collective-permute-start(bf16[144,512]{1,0:T(8,128)(2,1)S(1)} %get-tuple-element.14), channel_id=1, source_target_pairs={{0,2},{1,3},{2,0},{3,1},{4,6},{5,7},{6,4},{7,5}} | collective-permute-start | bytes 442376 | tf_op jit(solution)/shard_map/ppermute | solution.py:503
  54.9 1.0 %collective-permute-start.2 = (bf16[144,512]{1,0:T(8,128)(2,1)S(1)}, bf16[144,512]{1,0:T(8,128)(2,1)S(1)}, u32[]{:S(2)}, u32[]{:S(2)}) collective-permute-start(bf16[144,512]{1,0:T(8,128)(2,1)S(1)} %get-tuple-element.15), channel_id=1, source_target_pairs={{0,4},{1,5},{2,6},{3,7},{4,0},{5,1},{6,2},{7,3}} | collective-permute-start | bytes 442376 | tf_op jit(solution)/shard_map/ppermute | solution.py:503
  55.9 0.0 copy-done
  55.9 12.0 %caches.1 = (bf16[2,64,256,256]{3,2,1,0:T(8,128)(2,1)}, bf16[2,64,256,256]{3,2,1,0:T(8,128)(2,1)}) custom-call(s32[64]{0:T(128)S(1)} %copy-done, f32[2,64,256]{2,1,0:T(8,128)S(1)} %get-tuple-element.16.new_k, f32[2,64,256]{2,1,0:T(8,128)S(1)} %get-tuple-element.17.new_v, bf16[2,2,64,256,256]{4,3,2,1,0:T(8,128)(2,1)S(1)} %get-tuple-element.18.kv_all), custom_call_target="tpu_custom_call" | custom-call | tf_op jit(solution)/shard_map/caches/pallas_call | solution.py:507
  67.9 0.0 collective-permute-done.part_d
  68.0 0.0 collective-permute-done.1.part_x
  68.0 0.0 collective-permute-done.2.part_y
  68.0 1.0 %last.1 = bf16[144,512]{1,0:T(8,128)(2,1)} custom-call(f32[144,512]{1,0:T(8,128)S(1)} %get-tuple-element.12.base, bf16[144,512]{1,0:T(8,128)(2,1)S(1)} %collective-permute-done.part_d, bf16[144,512]{1,0:T(8,128)(2,1)S(1)} %collective-permute-done.1.part_x, bf16[144,512]{1,0:T(8,128)(2,1)S(1)} %collective-permute-done.2.part_y), custom_call_target="tpu_custom_call" | custom-call | tf_op jit(solution)/shard_map/last/pallas_call | solution.py:516
Async XLA Ops:
  0.6 55.3 %copy-start = (s32[64]{0:T(128)S(1)}, s32[64]{0:T(128)}, u32[]{:S(2)}) copy-start(s32[64]{0:T(128)} %lengths.1) | copy-start | bytes 772
  52.4 15.6 %collective-permute-start = (bf16[144,512]{1,0:T(8,128)(2,1)S(1)}, bf16[144,512]{1,0:T(8,128)(2,1)S(1)}, u32[]{:S(2)}, u32[]{:S(2)}) collective-permute-start(bf16[144,512]{1,0:T(8,128)(2,1)S(1)} %get-tuple-element.13), channel_id=1, source_target_pairs={{0,6},{1,7},{2,4},{3,5},{4,2},{5,3},{6,0},{7,1}} | collective-permute-start | bytes 442376 | tf_op jit(solution)/shard_map/ppermute | solution.py:503
  53.7 14.2 %collective-permute-start.1 = (bf16[144,512]{1,0:T(8,128)(2,1)S(1)}, bf16[144,512]{1,0:T(8,128)(2,1)S(1)}, u32[]{:S(2)}, u32[]{:S(2)}) collective-permute-start(bf16[144,512]{1,0:T(8,128)(2,1)S(1)} %get-tuple-element.14), channel_id=1, source_target_pairs={{0,2},{1,3},{2,0},{3,1},{4,6},{5,7},{6,4},{7,5}} | collective-permute-start | bytes 442376 | tf_op jit(solution)/shard_map/ppermute | solution.py:503
  54.9 13.1 %collective-permute-start.2 = (bf16[144,512]{1,0:T(8,128)(2,1)S(1)}, bf16[144,512]{1,0:T(8,128)(2,1)S(1)}, u32[]{:S(2)}, u32[]{:S(2)}) collective-permute-start(bf16[144,512]{1,0:T(8,128)(2,1)S(1)} %get-tuple-element.15), channel_id=1, source_target_pairs={{0,4},{1,5},{2,6},{3,7},{4,0},{5,1},{6,2},{7,3}} | collective-permute-start | bytes 442376 | tf_op jit(solution)/shard_map/ppermute | solution.py:503
